TPU v7x, 8 devices: a whole 2x2x1 slice. The times are simulated.
8 devices in a mesh: dp: 1 (over z), tp: 8 (over x, y, core).
Axes of the slice: x: 2, y: 2, z: 1, core: 2. Of those that a mesh axis runs over, the one named last changes fastest.
Arguments:
- x: bfloat16 [64, 2048], P('dp')
- k_cache: bfloat16 [64, 4096, 16, 128], P('dp', None, 'tp')
- v_cache: bfloat16 [64, 4096, 16, 128], P('dp', None, 'tp')
- gain_a: bfloat16 [2048], replicated
- wq: bfloat16 [2048, 2048], P(None, 'tp')
- wo: bfloat16 [2048, 2048], P('tp')
- gain_m: bfloat16 [2048], replicated
- w_gate: bfloat16 [2048, 8192], P(None, 'tp')
- w_up: bfloat16 [2048, 8192], P(None, 'tp')
- w_down: bfloat16 [8192, 2048], P('tp')
Outputs:
- output: bfloat16 [64, 2048], P('dp')
All inputs are finite; a program needn't handle non-finite values.
Results may differ from a plain program's by a relative error of at most 0.017.
Values are sent between devices in bfloat16 or wider.
A program may use at most 2 GiB of HBM per device.

v0:
```python
import jax
import jax.numpy as jnp
from jax import lax
from jax.sharding import PartitionSpec as P

HEAD = 128
THETA = 10000


def normed(x, gain):
    wide = x.astype(jnp.float32)
    scale = lax.rsqrt(jnp.mean(wide * wide, -1, keepdims=True) + 1e-6)
    return (wide * scale * gain.astype(jnp.float32)).astype(jnp.bfloat16)


def turned(t, place, theta):
    half = t.shape[-1] // 2
    angle = place.astype(jnp.float32)[:, None] * theta ** (-jnp.arange(half, dtype=jnp.float32) / half)
    cos, sin = jnp.cos(angle)[:, None], jnp.sin(angle)[:, None]
    a, b = t[..., :half].astype(jnp.float32), t[..., half:].astype(jnp.float32)
    return jnp.concatenate([a * cos - b * sin, b * cos + a * sin], -1).astype(jnp.bfloat16)


def matmul(a, w):
    return jnp.dot(a, w, preferred_element_type=jnp.float32).astype(jnp.bfloat16)


def einsum(form, a, b):
    return jnp.einsum(form, a.astype(jnp.float32), b.astype(jnp.float32))


def seen_by(a, wq, k_cache, v_cache, head, theta):
    batch, cache, kv_heads = k_cache.shape[:3]
    place = jnp.full((batch,), cache - 1)
    q = turned(matmul(a, wq).reshape(batch, -1, head), place, theta).reshape(batch, kv_heads, -1, head)
    scores = einsum("bgsd,bugd->bgsu", q, k_cache) * head**-0.5
    weights = jax.nn.softmax(scores, -1).astype(jnp.bfloat16)
    return einsum("bgsu,bugd->bgsd", weights, v_cache).astype(jnp.bfloat16).reshape(batch, -1)


def hidden_of(b, w_gate, w_up):
    gate = jnp.dot(b, w_gate, preferred_element_type=jnp.float32)
    up = jnp.dot(b, w_up, preferred_element_type=jnp.float32)
    return (jax.nn.silu(gate) * up).astype(jnp.bfloat16)


def solution(mesh):
    def added(t, term):
        return (t.astype(jnp.float32) + lax.psum(term.astype(jnp.bfloat16), "tp").astype(jnp.float32)).astype(jnp.bfloat16)

    def step(x, k_cache, v_cache, gain_a, wq, wo, gain_m, w_gate, w_up, w_down):
        seen = seen_by(normed(x, gain_a), wq, k_cache, v_cache, HEAD, THETA)
        h = added(x, jnp.dot(seen, wo, preferred_element_type=jnp.float32))
        return added(h, jnp.dot(hidden_of(normed(h, gain_m), w_gate, w_up), w_down, preferred_element_type=jnp.float32))

    states, cache, columns, rows_of = P("dp", None), P("dp", None, "tp", None), P(None, "tp"), P("tp", None)
    return jax.shard_map(
        step,
        mesh=mesh,
        in_specs=(states, cache, cache, P(None), columns, rows_of, P(None), columns, columns, rows_of),
        out_specs=states,
        check_vma=False,
    )
```

profile of v0, /device:TPU:0, one launch (start us, length us, event | category | flops | bytes accessed | tf_op | source)
XLA Modules:
  0.0 229.5 jit_solution(15003612536475200414)
XLA Ops:
  6.5 0.0 copy-start
  6.5 0.0 all-reduce.3.cloned.1.call-start
  6.6 0.8 convert_element_type.66
  7.4 1.1 fusion.15
  8.5 1.7 convolution_convert_fusion.2
  10.2 0.1 fusion.51
  10.3 0.1 maximum_bitcast_fusion
  10.4 61.3 %fusion.4 = f32[64,2,1,4096]{3,2,1,0:T(1,128)S(1)} fusion(bf16[64,4096,2,128]{3,2,1,0:T(2,128)(2,1)} %param.11, bf16[64,2,128,1]{2,0,1,3:T(8,128)(2,1)S(1)} %maximum_bitcast_fusion), kind=kOutput, calls=%fused_computation.4 | convolution fusion | flops 134217728 | bytes 136347648 | tf_op jit(solution)/shard_map/bgsd,bugd->bgsu/dot_general | solution.py:29
  71.7 3.7 %fusion.10 = bf16[64,2,4096,1]{2,0,1,3:T(8,128)(2,1)} fusion(f32[64,2,1,4096]{3,2,1,0:T(1,128)S(1)} %fusion.4), kind=kOutput, calls=%fused_computation.10 | output fusion | flops 2105598 | bytes 3145728 | tf_op jit(solution)/shard_map/div | solution.py:37
  75.5 0.0 copy-start.2
  75.5 0.0 copy-start.1
  75.5 46.7 %fusion.2 = f32[64,2,1,128]{3,2,1,0:T(1,128)S(1)} fusion(bf16[64,4096,2,128]{3,2,1,0:T(2,128)(2,1)} %param.12, bf16[64,2,4096,1]{2,0,1,3:T(8,128)(2,1)} %fusion.10), kind=kOutput, calls=%fused_computation.2 | convolution fusion | flops 134217728 | bytes 135331840 | tf_op jit(solution)/shard_map/bgsu,bugd->bgsd/dot_general | solution.py:29
  122.2 0.0 copy-done
  122.2 1.0 convolution_convert_fusion
  123.2 0.0 all-reduce.3.cloned.1.call-update
  123.2 0.0 all-reduce.5.cloned.1.call-start
  123.3 0.0 copy-done.2
  123.3 45.5 %all-reduce.3.cloned.1.call-done = bf16[64,2048]{1,0:T(8,128)(2,1)} async-done(((bf16[64,2048]{1,0:T(8,128)(2,1)}), bf16[64,2048]{1,0:T(8,128)(2,1)}) %all-reduce.3.cloned.1.call-update) | async-done | bytes 262160 | tf_op jit(solution)/shard_map/psum | solution.py:49
  168.8 0.0 copy-done.1
  168.8 1.1 fusion.19
  170.0 3.1 %fusion.34 = f32[64,1024]{1,0:T(8,128)S(1)} fusion(bf16[2048,1024]{1,0:T(8,128)(2,1)} %param.17, bf16[64,2048]{1,0:T(8,128)(2,1)S(1)} %get-tuple-element.6, f32[2048]{0:T(1024)S(1)} %convert_element_type.77, f32[64]{0:T(128)S(1)} %add_rsqrt_fusion), kind=kOutput, calls=%fused_computation.46 | convolution fusion | flops 268959744 | bytes 4727040 | tf_op jit(solution)/shard_map/dot_general | solution.py:42
  173.0 5.8 %convolution_convert_fusion.1 = bf16[64,2048]{1,0:T(8,128)(2,1)} fusion(bf16[1024,2048]{1,0:T(8,128)(2,1)} %param.19, bf16[2048,1024]{1,0:T(8,128)(2,1)} %param.18, f32[64,1024]{1,0:T(8,128)S(1)} %fusion.34, bf16[64,2048]{1,0:T(8,128)(2,1)S(1)} %get-tuple-element.6, f32[2048]{0:T(1024)S(1)} %convert_element_type.77, f32[64]{0:T(128)S(1)} %add_rsqrt_fusion), kind=kOutput, calls=%fused_computation.12 | convolution fusion | flops 537919488 | bytes 9183488 | tf_op jit(solution)/shard_map/dot_general | solution.py:54
  178.9 0.0 all-reduce.5.cloned.1.call-update
  178.9 42.1 %all-reduce.5.cloned.1.call-done = bf16[64,2048]{1,0:T(8,128)(2,1)} async-done(((bf16[64,2048]{1,0:T(8,128)(2,1)}), bf16[64,2048]{1,0:T(8,128)(2,1)}) %all-reduce.5.cloned.1.call-update) | async-done | bytes 262160 | tf_op jit(solution)/shard_map/psum | solution.py:49
  220.9 1.7 fusion.22
  (7 shorter events, 0.1 us)
Async XLA Ops:
  6.5 115.7 %copy-start = (bf16[256,2048]{1,0:T(8,128)(2,1)S(1)}, bf16[256,2048]{1,0:T(8,128)(2,1)}, u32[]{:S(2)}) copy-start(bf16[256,2048]{1,0:T(8,128)(2,1)} %param.15) | copy-start | bytes 3145732
  6.5 162.3 %all-reduce.3.cloned.1.call-start = ((), (), s32[]{:S(2)}) async-start(), calls=%async_computation | async-start | bytes 524288 | tf_op jit(solution)/shard_map/psum | solution.py:49
  75.5 47.8 %copy-start.2 = (bf16[2048]{0:T(1024)(128)(2,1)S(1)}, bf16[2048]{0:T(1024)(128)(2,1)}, u32[]{:S(2)}) copy-start(bf16[2048]{0:T(1024)(128)(2,1)} %param.16) | copy-start | bytes 12292
  75.5 93.3 %copy-start.1 = (bf16[64,2048]{1,0:T(8,128)(2,1)S(1)}, bf16[64,2048]{1,0:T(8,128)(2,1)}, u32[]{:S(2)}) copy-start(bf16[64,2048]{1,0:T(8,128)(2,1)} %param.10) | copy-start | bytes 786436
  123.2 97.7 %all-reduce.5.cloned.1.call-start = ((), (), s32[]{:S(2)}) async-start(), calls=%async_computation.1 | async-start | bytes 524288 | tf_op jit(solution)/shard_map/psum | solution.py:49
Sparse Core Ops, SparseCore 0:
  123.4 45.3 all-reduce.2
  179.0 41.8 all-reduce.4
where the time goes:
time: 230 us; the launch traced here: 229 us
  matrix products  120 us (52%)
  waiting for transfers between devices  87.6 us (38%)
  between operations  13.5 us (6%)
  other arithmetic  8.66 us (4%)
    dot_general x2, matrix products, einsum(): return jnp.einsum(form, a.astype(jnp.float32), b.astype(jnp.float32))  108 us
    psum x2, waiting for transfers between devices, added(): lax.psum(term.astype(jnp.bfloat16), 'tp').astype(jnp.float32)  87.5 us
    dot_general x1, matrix products, step(): jnp.dot(hidden_of(normed(h, gain_m), w_gate, w_up), w_down, preferred_ele...  5.81 us
  transfers between devices with their start and end apart: 2, of which 2 were waited for; matrix products, arithmetic and copies ran while one was open for 0% of the time, Pallas kernels for 0%

commit v1 on v0

--- a/solution.py
+++ b/solution.py
@@ -1,10 +1,17 @@
+import functools
+
 import jax
 import jax.numpy as jnp
 from jax import lax
+from jax.experimental import pallas as pl
+from jax.experimental.pallas import tpu as pltpu
 from jax.sharding import PartitionSpec as P
 
 HEAD = 128
 THETA = 10000
+F32, BF16 = jnp.float32, jnp.bfloat16
+LOG2E = 1.4426950408889634
+NK = NV = 6
 
 
 def normed(x, gain):
@@ -25,23 +32,122 @@
     return jnp.dot(a, w, preferred_element_type=jnp.float32).astype(jnp.bfloat16)
 
 
-def einsum(form, a, b):
-    return jnp.einsum(form, a.astype(jnp.float32), b.astype(jnp.float32))
+def hidden_of(b, w_gate, w_up):
+    gate = jnp.dot(b, w_gate, preferred_element_type=jnp.float32)
+    up = jnp.dot(b, w_up, preferred_element_type=jnp.float32)
+    return (jax.nn.silu(gate) * up).astype(jnp.bfloat16)
+
+
+def scores_of(q_ref, kbuf, s_ref, b, slot, par, tiles):
+    row = q_ref[pl.ds(b, 1), :]
+    q0 = jnp.broadcast_to(row[:, :HEAD], (16, HEAD))
+    q1 = jnp.broadcast_to(row[:, HEAD:], (16, HEAD))
+    r = lax.broadcasted_iota(jnp.int32, (16, HEAD), 0)
+    q = jnp.where((r & 1) == 0, q0, q1)
+    first = (r & 2) == 0
+    lhs = jnp.concatenate([jnp.where(first, q, 0.0), jnp.where(first, 0.0, q)], 1).astype(BF16)
+    for j in range(tiles):
+        ka = kbuf[slot, 512 * j : 512 * j + 256, :]
+        kb = kbuf[slot, 512 * j + 256 : 512 * j + 512, :]
+        s = lax.dot_general(lhs, jnp.concatenate([ka, kb], 1), (((1,), (1,)), ((), ())), preferred_element_type=F32)
+        s_ref[par, :, 256 * j : 256 * j + 256] = s[:8]
+
+
+def seen_from(s_ref, vbuf, seen_ref, b, slot, par, tiles):
+    r = lax.broadcasted_iota(jnp.int32, (8, 256), 0)
+    c = lax.broadcasted_iota(jnp.int32, (8, 256), 1)
+    mine = (r & 1) == (c & 1)
+    t = [jnp.where(mine, s_ref[par, :, 256 * j : 256 * j + 256], -1e30) for j in range(tiles)]
+    m = functools.reduce(jnp.maximum, t)
+    m = jnp.max(jnp.maximum(m[:, :128], m[:, 128:]), 1, keepdims=True)
+    m = jnp.broadcast_to(m, (8, 128))
+    m = jnp.maximum(m, pltpu.roll(m, 2, 0))
+    m = jnp.concatenate([m, m], 1)
+    k = HEAD**-0.5 * LOG2E
+    p = [jnp.exp2((x - m) * k) for x in t]
+    l = functools.reduce(jnp.add, p)
+    l = jnp.sum(l[:, :128] + l[:, 128:], 1, keepdims=True)
+    l = jnp.broadcast_to(l, (8, 128))
+    l = l + pltpu.roll(l, 2, 0)
+    inv = 1.0 / l
+    inv = jnp.concatenate([inv, inv], 1)
+    o = jnp.zeros((16, 256), F32)
+    for j in range(tiles):
+        w = p[j] * inv
+        w = jnp.concatenate([w, w], 0).astype(BF16)
+        va = vbuf[slot, 512 * j : 512 * j + 256, :]
+        vb = vbuf[slot, 512 * j + 256 : 512 * j + 512, :]
+        o = o + jnp.dot(w, jnp.concatenate([va, vb], 1), preferred_element_type=F32)
+    o = o[:8]
+    o = o[:, :128] + pltpu.roll(o[:, 128:], 6, 0)
+    seen_ref[b] = o
+
+
+def attention(q_ref, k_ref, v_ref, out_ref, kbuf, vbuf, s_ref, seen_ref, ksem, vsem):
+    n = k_ref.shape[0]
+    tiles = k_ref.shape[1] // 512
+
+    def kcopy(b, slot):
+        return pltpu.make_async_copy(k_ref.at[b], kbuf.at[slot], ksem.at[slot])
+
+    def vcopy(b, slot):
+        return pltpu.make_async_copy(v_ref.at[b], vbuf.at[slot], vsem.at[slot])
+
+    for s in range(NK):
+        kcopy(s, s).start()
+        vcopy(s, s).start()
+    kcopy(0, 0).wait()
+    scores_of(q_ref, kbuf, s_ref, 0, 0, 0, tiles)
+    kcopy(NK, 0).start()
+
+    def body(i, carry):
+        kslot, vslot = lax.rem(i + 1, NK), lax.rem(i, NV)
+        kcopy(i + 1, kslot).wait()
+        vcopy(i, vslot).wait()
+        par = lax.rem(i, 2)
+        scores_of(q_ref, kbuf, s_ref, i + 1, kslot, 1 - par, tiles)
+        seen_from(s_ref, vbuf, seen_ref, i, vslot, par, tiles)
+
+        @pl.when(i + 1 + NK < n)
+        def _():
+            kcopy(i + 1 + NK, kslot).start()
+
+        @pl.when(i + NV < n)
+        def _():
+            vcopy(i + NV, vslot).start()
+
+        return carry
+
+    lax.fori_loop(0, n - 1, body, 0)
+    vcopy(n - 1, (n - 1) % NV).wait()
+    seen_from(s_ref, vbuf, seen_ref, n - 1, (n - 1) % NV, (n - 1) % 2, tiles)
+    out_ref[...] = jnp.concatenate([seen_ref[:, 0, :], seen_ref[:, 1, :]], 1).astype(BF16)
+
+
+def attend(q, k, v):
+    n, rows, head = k.shape
+    return pl.pallas_call(
+        attention,
+        out_shape=jax.ShapeDtypeStruct((n, 2 * head), BF16),
+        in_specs=[pl.BlockSpec(memory_space=pltpu.VMEM)] + [pl.BlockSpec(memory_space=pl.ANY)] * 2,
+        out_specs=pl.BlockSpec(memory_space=pltpu.VMEM),
+        scratch_shapes=[
+            pltpu.VMEM((NK, rows, head), BF16),
+            pltpu.VMEM((NV, rows, head), BF16),
+            pltpu.VMEM((2, 8, rows // 2), F32),
+            pltpu.VMEM((n, 8, head), F32),
+            pltpu.SemaphoreType.DMA((NK,)),
+            pltpu.SemaphoreType.DMA((NV,)),
+        ],
+        compiler_params=pltpu.CompilerParams(vmem_limit_bytes=60 << 20),
+    )(q, k, v)
 
 
 def seen_by(a, wq, k_cache, v_cache, head, theta):
     batch, cache, kv_heads = k_cache.shape[:3]
     place = jnp.full((batch,), cache - 1)
-    q = turned(matmul(a, wq).reshape(batch, -1, head), place, theta).reshape(batch, kv_heads, -1, head)
-    scores = einsum("bgsd,bugd->bgsu", q, k_cache) * head**-0.5
-    weights = jax.nn.softmax(scores, -1).astype(jnp.bfloat16)
-    return einsum("bgsu,bugd->bgsd", weights, v_cache).astype(jnp.bfloat16).reshape(batch, -1)
-
-
-def hidden_of(b, w_gate, w_up):
-    gate = jnp.dot(b, w_gate, preferred_element_type=jnp.float32)
-    up = jnp.dot(b, w_up, preferred_element_type=jnp.float32)
-    return (jax.nn.silu(gate) * up).astype(jnp.bfloat16)
+    q = turned(matmul(a, wq).reshape(batch, -1, head), place, theta).reshape(batch, -1)
+    return attend(q.astype(F32), k_cache.reshape(batch, -1, head), v_cache.reshape(batch, -1, head))
 
 
 def solution(mesh):

time: 230 us -> 201 us (0.87)
  matrix products: 120 us -> 12.3 us
  Pallas kernels: 0 us -> 81.9 us
  other arithmetic: 8.66 us -> 5.54 us
    dot_general x2 -> x0, matrix products: 108 us -> none  [einsum(): return jnp.einsum(form, a.astype(jnp.float32), b.astype(jnp.float32))]
    pallas_call x0 -> x1, Pallas kernels: none -> 81.9 us  [attend(): pl.pallas_call(attention, out_shape=jax.ShapeDtypeStruct((n, 2 * head), B...]
    div x1 -> x0, other arithmetic: 3.73 us -> none  [seen_by(): weights = jax.nn.softmax(scores, -1).astype(jnp.bfloat16)]
where the time goes in v1:
time: 201 us
  waiting for transfers between devices  87.6 us (44%)
  Pallas kernels  81.9 us (41%)
  between operations  13.5 us (7%)
  matrix products  12.3 us (6%)
  other arithmetic  5.54 us (3%)
    psum x2, waiting for transfers between devices, added(): lax.psum(term.astype(jnp.bfloat16), 'tp').astype(jnp.float32)  87.5 us
    pallas_call x1, Pallas kernels, attend(): pl.pallas_call(attention, out_shape=jax.ShapeDtypeStruct((n, 2 * head), B...  81.9 us
    dot_general x1, matrix products, step(): jnp.dot(hidden_of(normed(h, gain_m), w_gate, w_up), w_down, preferred_ele...  5.81 us
  transfers between devices with their start and end apart: 2, of which 2 were waited for; matrix products, arithmetic and copies ran while one was open for 0% of the time, Pallas kernels for 0%

profile of v1, /device:TPU:0, one launch (start us, length us, event | category | flops | bytes accessed | tf_op | source)
XLA Modules:
  0.0 201.0 jit_solution(14694933918271539881)
XLA Ops:
  6.5 0.0 copy-start
  6.5 0.0 all-reduce.3.cloned.1.call-start
  6.6 1.2 fusion.1
  7.8 0.7 convert_element_type.59
  8.5 1.6 convolution_convert_fusion.2
  10.2 0.1 fusion.30
  10.3 0.7 copy_bitcast_fusion.q_ref
  11.0 0.0 copy-start.2
  11.0 0.0 copy-start.1
  11.0 81.9 %shard_map.100 = bf16[64,256]{1,0:T(8,128)(2,1)} custom-call(f32[64,256]{1,0:T(8,128)} %copy_bitcast_fusion.q_ref, bf16[64,8192,128]{2,1,0:T(8,128)(2,1)} %bitcast.k_ref, bf16[64,8192,128]{2,1,0:T(8,128)(2,1)} %bitcast.1.v_ref), custom_call_target="tpu_custom_call" | custom-call | tf_op jit(solution)/shard_map/pallas_call | solution.py:129
  93.0 0.0 copy-done
  93.0 1.8 convolution_convert_fusion
  94.7 0.0 all-reduce.3.cloned.1.call-update
  94.7 0.0 all-reduce.5.cloned.1.call-start
  94.8 0.0 copy-done.2
  94.8 45.5 %all-reduce.3.cloned.1.call-done = bf16[64,2048]{1,0:T(8,128)(2,1)} async-done(((bf16[64,2048]{1,0:T(8,128)(2,1)}), bf16[64,2048]{1,0:T(8,128)(2,1)}) %all-reduce.3.cloned.1.call-update) | async-done | bytes 262160 | tf_op jit(solution)/shard_map/psum | solution.py:155
  140.3 0.0 copy-done.1
  140.3 1.1 fusion.5
  141.5 3.1 %fusion.20 = f32[64,1024]{1,0:T(8,128)S(1)} fusion(bf16[2048,1024]{1,0:T(8,128)(2,1)} %param.17, bf16[64,2048]{1,0:T(8,128)(2,1)S(1)} %get-tuple-element.6, f32[2048]{0:T(1024)S(1)} %convert_element_type.70, f32[64]{0:T(128)S(1)} %add_rsqrt_fusion), kind=kOutput, calls=%fused_computation.31 | convolution fusion | flops 268959744 | bytes 4727040 | tf_op jit(solution)/shard_map/dot_general | solution.py:36
  144.5 5.8 %convolution_convert_fusion.1 = bf16[64,2048]{1,0:T(8,128)(2,1)} fusion(bf16[1024,2048]{1,0:T(8,128)(2,1)} %param.19, bf16[2048,1024]{1,0:T(8,128)(2,1)} %param.18, f32[64,1024]{1,0:T(8,128)S(1)} %fusion.20, bf16[64,2048]{1,0:T(8,128)(2,1)S(1)} %get-tuple-element.6, f32[2048]{0:T(1024)S(1)} %convert_element_type.70, f32[64]{0:T(128)S(1)} %add_rsqrt_fusion), kind=kOutput, calls=%fused_computation.1 | convolution fusion | flops 537919488 | bytes 9183488 | tf_op jit(solution)/shard_map/dot_general | solution.py:160
  150.4 0.0 all-reduce.5.cloned.1.call-update
  150.4 42.1 %all-reduce.5.cloned.1.call-done = bf16[64,2048]{1,0:T(8,128)(2,1)} async-done(((bf16[64,2048]{1,0:T(8,128)(2,1)}), bf16[64,2048]{1,0:T(8,128)(2,1)}) %all-reduce.5.cloned.1.call-update) | async-done | bytes 262160 | tf_op jit(solution)/shard_map/psum | solution.py:155
  192.4 1.7 fusion.8
  (6 shorter events, 0.1 us)
Async XLA Ops:
  6.5 86.4 %copy-start = (bf16[256,2048]{1,0:T(8,128)(2,1)S(1)}, bf16[256,2048]{1,0:T(8,128)(2,1)}, u32[]{:S(2)}) copy-start(bf16[256,2048]{1,0:T(8,128)(2,1)} %param.15) | copy-start | bytes 3145732
  6.5 133.8 %all-reduce.3.cloned.1.call-start = ((), (), s32[]{:S(2)}) async-start(), calls=%async_computation | async-start | bytes 524288 | tf_op jit(solution)/shard_map/psum | solution.py:155
  11.0 83.8 %copy-start.2 = (bf16[2048]{0:T(1024)(128)(2,1)S(1)}, bf16[2048]{0:T(1024)(128)(2,1)}, u32[]{:S(2)}) copy-start(bf16[2048]{0:T(1024)(128)(2,1)} %param.16) | copy-start | bytes 12292
  11.0 129.3 %copy-start.1 = (bf16[64,2048]{1,0:T(8,128)(2,1)S(1)}, bf16[64,2048]{1,0:T(8,128)(2,1)}, u32[]{:S(2)}) copy-start(bf16[64,2048]{1,0:T(8,128)(2,1)} %param.10) | copy-start | bytes 786436
  94.7 97.7 %all-reduce.5.cloned.1.call-start = ((), (), s32[]{:S(2)}) async-start(), calls=%async_computation.1 | async-start | bytes 524288 | tf_op jit(solution)/shard_map/psum | solution.py:155
Sparse Core Ops, SparseCore 0:
  94.9 45.3 all-reduce.2
  150.5 41.8 all-reduce.4

commit v2 on v1

v2 whole, which is shorter than its diff:
```python
import functools

import jax
import jax.numpy as jnp
import numpy as np
from jax import lax
from jax.experimental import pallas as pl
from jax.experimental.pallas import tpu as pltpu
from jax.sharding import PartitionSpec as P

HEAD = 128
THETA = 10000
F32, BF16 = jnp.float32, jnp.bfloat16
LOG2E = 1.4426950408889634
NK = NV = 6
G = 8
RS_H, AG_H, RS_Y, AG_Y = range(4)


def normed(wide, gain):
    gain = gain.astype(F32)
    gain = jnp.concatenate([gain[c : c + 1] for c in range(gain.shape[0])], 1)
    scale = lax.rsqrt(jnp.mean(wide * wide, -1, keepdims=True) + 1e-6)
    return (wide * scale * gain).astype(BF16)


def twice(t):
    return jnp.concatenate([t, t], 0).astype(BF16)


def scores_of(q_ref, kbuf, s_ref, b, slot, par):
    row = q_ref[pl.ds(b, 1), :]
    q0 = jnp.broadcast_to(row[:, :HEAD], (16, HEAD))
    q1 = jnp.broadcast_to(row[:, HEAD:], (16, HEAD))
    r = lax.broadcasted_iota(jnp.int32, (16, HEAD), 0)
    q = jnp.where((r & 1) == 0, q0, q1)
    first = (r & 2) == 0
    lhs = jnp.concatenate([jnp.where(first, q, 0.0), jnp.where(first, 0.0, q)], 1).astype(BF16)
    for j in range(kbuf.shape[1] // 512):
        ka = kbuf[slot, 512 * j : 512 * j + 256, :]
        kb = kbuf[slot, 512 * j + 256 : 512 * j + 512, :]
        s = lax.dot_general(lhs, jnp.concatenate([ka, kb], 1), (((1,), (1,)), ((), ())), preferred_element_type=F32)
        s_ref[par, :, 256 * j : 256 * j + 256] = s[:8]


def seen_from(s_ref, vbuf, seen_ref, b, slot, par):
    tiles = vbuf.shape[1] // 512
    r = lax.broadcasted_iota(jnp.int32, (8, 256), 0)
    c = lax.broadcasted_iota(jnp.int32, (8, 256), 1)
    mine = (r & 1) == (c & 1)
    t = [jnp.where(mine, s_ref[par, :, 256 * j : 256 * j + 256], -1e30) for j in range(tiles)]
    m = functools.reduce(jnp.maximum, t)
    m = jnp.max(jnp.maximum(m[:, :128], m[:, 128:]), 1, keepdims=True)
    m = jnp.broadcast_to(m, (8, 128))
    m = jnp.maximum(m, pltpu.roll(m, 2, 0))
    m = jnp.concatenate([m, m], 1)
    k = HEAD**-0.5 * LOG2E
    p = [jnp.exp2((x - m) * k) for x in t]
    l = functools.reduce(jnp.add, p)
    l = jnp.sum(l[:, :128] + l[:, 128:], 1, keepdims=True)
    l = jnp.broadcast_to(l, (8, 128))
    l = l + pltpu.roll(l, 2, 0)
    inv = 1.0 / l
    inv = jnp.concatenate([inv, inv], 1)
    o = jnp.zeros((16, 256), F32)
    for j in range(tiles):
        va = vbuf[slot, 512 * j : 512 * j + 256, :]
        vb = vbuf[slot, 512 * j + 256 : 512 * j + 512, :]
        o = o + jnp.dot(twice(p[j] * inv), jnp.concatenate([va, vb], 1), preferred_element_type=F32)
    o = o[:8]
    seen_ref[b] = o[:, :128] + pltpu.roll(o[:, 128:], 6, 0)


def layer(
    n_dev, x_ref, k_ref, v_ref, ga_ref, wq_ref, wo_ref, gm_ref, wg_ref, wu_ref, wd_ref, turn_ref, out_ref,
    kbuf, vbuf, x_v, xc_v, ga_v, gm_v, turn_v, wq_v, wo_v, wg_v, wu_v, wd_v,
    q_v, s_v, seen_v, own_v, hsend, hrecv, hmine, hfull, ysend, yrecv, ymine,
    ksem, vsem, wsem, outsem, send_sem, recv_sem,
):
    me = lax.axis_index("tp")
    n = k_ref.shape[0]
    groups = n // G
    d = x_ref.shape[2]
    cols = d // n_dev
    mine = pl.ds(pl.multiple_of(me * cols, cols), cols)
    peers = [lax.rem(me + j, n_dev) for j in range(1, n_dev)]
    sources = [lax.rem(me + n_dev - j, n_dev) for j in range(1, n_dev)]

    barrier = pltpu.get_barrier_semaphore()
    for peer in peers:
        pl.semaphore_signal(barrier, inc=1, device_id={"tp": peer}, device_id_type=pl.DeviceIdType.MESH)

    loads = [
        pltpu.make_async_copy(src, dst, wsem.at[i])
        for i, (src, dst) in enumerate(
            [
                (x_ref, x_v),
                (ga_ref, ga_v),
                (turn_ref, turn_v),
                (wq_ref, wq_v),
                (x_ref.at[:, :, mine], xc_v),
                (gm_ref, gm_v),
                (wo_ref, wo_v),
                (wg_ref, wg_v),
                (wu_ref, wu_v),
                (wd_ref, wd_v),
            ]
        )
    ]

    def kcopy(b, slot):
        return pltpu.make_async_copy(k_ref.at[b], kbuf.at[slot], ksem.at[slot])

    def vcopy(b, slot):
        return pltpu.make_async_copy(v_ref.at[b], vbuf.at[slot], vsem.at[slot])

    def scatter(phase, buf, into, peer, source):
        return pltpu.make_async_remote_copy(
            src_ref=buf.at[peer],
            dst_ref=into.at[source],
            send_sem=send_sem.at[phase, peer],
            recv_sem=recv_sem.at[phase, source],
            device_id={"tp": peer},
            device_id_type=pl.DeviceIdType.MESH,
        )

    def gather(phase, chunk, into, peer, source):
        at = pl.ds(pl.multiple_of(source * cols, cols), cols)
        return pltpu.make_async_remote_copy(
            src_ref=chunk,
            dst_ref=into.at[:, at],
            send_sem=send_sem.at[phase, peer],
            recv_sem=recv_sem.at[phase, source],
            device_id={"tp": peer},
            device_id_type=pl.DeviceIdType.MESH,
        )

    def summed(recv, own):
        total = own
        for source in sources:
            total = total + recv[source].astype(F32)
        return total

    def term(g, out, send, recv, phase):
        for i in range(n_dev):
            own_v[i] = out[:G, cols * i : cols * (i + 1)]
            send[i] = out[:G, cols * i : cols * (i + 1)].astype(BF16)
        for peer in peers:
            scatter(phase, send, recv, peer, me).start()

    def arrived(phase, send, recv):
        for source in sources:
            scatter(phase, send, recv, me, source).wait_recv()
        for peer in peers:
            scatter(phase, send, recv, peer, me).wait_send()

    def attended(g):
        @pl.when(g == 0)
        def _():
            loads[6].wait()

        rows = pl.ds(g * G, G)
        seen = jnp.concatenate([seen_v[rows, 0, :], seen_v[rows, 1, :]], 1)
        out = jnp.dot(twice(seen), wo_v[...], preferred_element_type=F32)
        term(g, out, hsend, hrecv, RS_H)

    def half(g):
        arrived(RS_H, hsend, hrecv)
        h = (xc_v[g].astype(F32) + summed(hrecv, own_v[me])).astype(BF16)
        hmine[...] = h
        hfull[:, mine] = h
        for peer in peers:
            gather(AG_H, hmine, hfull, peer, me).start()

    def through(g):
        @pl.when(g == 0)
        def _():
            for load in loads[7:]:
                load.wait()

        for source in sources:
            gather(AG_H, hmine, hfull, me, source).wait_recv()
        for peer in peers:
            gather(AG_H, hmine, hfull, peer, me).wait_send()
        b = twice(normed(hfull[...].astype(F32), gm_v[...]).astype(F32))
        gate = jnp.dot(b, wg_v[...], preferred_element_type=F32)
        up = jnp.dot(b, wu_v[...], preferred_element_type=F32)
        out = jnp.dot((jax.nn.silu(gate) * up).astype(BF16), wd_v[...], preferred_element_type=F32)
        term(g, out, ysend, yrecv, RS_Y)

    def whole(g):
        arrived(RS_Y, ysend, yrecv)
        ymine[...] = (hmine[...].astype(F32) + summed(yrecv, own_v[me])).astype(BF16)
        for peer in peers:
            gather(AG_Y, ymine, out_ref.at[g], peer, me).start()
        pltpu.make_async_copy(ymine, out_ref.at[g, :, mine], outsem).start()

    def done(g):
        for source in sources:
            gather(AG_Y, ymine, out_ref.at[g], me, source).wait_recv()
        for peer in peers:
            gather(AG_Y, ymine, out_ref.at[g], peer, me).wait_send()
        pltpu.make_async_copy(ymine, out_ref.at[g, :, mine], outsem).wait()

    for load in loads[:4]:
        load.start()
    for s in range(NK):
        kcopy(s, s).start()
        vcopy(s, s).start()
    for load in loads[4:]:
        load.start()

    for load in loads[:4]:
        load.wait()
    wide = jnp.concatenate([x_v[g] for g in range(groups)], 0).astype(F32)
    q = jnp.dot(normed(wide, ga_v[...]), wq_v[...], preferred_element_type=F32).astype(BF16).astype(F32)
    for i in range(2):
        t = q[:, HEAD * i : HEAD * (i + 1)]
        t = t * turn_v[0:1, :] + pltpu.roll(t, HEAD // 2, 1) * turn_v[1:2, :]
        q_v[:, HEAD * i : HEAD * (i + 1)] = t.astype(BF16).astype(F32)
    loads[4].wait()
    loads[5].wait()
    pl.semaphore_wait(barrier, n_dev - 1)

    kcopy(0, 0).wait()
    scores_of(q_v, kbuf, s_v, 0, 0, 0)
    kcopy(NK, 0).start()

    def sequence(i, carry):
        kslot, vslot = lax.rem(i + 1, NK), lax.rem(i, NV)
        kcopy(i + 1, kslot).wait()
        vcopy(i, vslot).wait()
        par = lax.rem(i, 2)
        scores_of(q_v, kbuf, s_v, i + 1, kslot, 1 - par)
        seen_from(s_v, vbuf, seen_v, i, vslot, par)

        @pl.when(i + 1 + NK < n)
        def _():
            kcopy(i + 1 + NK, kslot).start()

        @pl.when(i + NV < n)
        def _():
            vcopy(i + NV, vslot).start()

        return carry

    steps = (half, through, whole, done)
    each = G // len(steps)

    def group(g, carry):
        for j, step in enumerate(steps):
            lax.fori_loop(g * G + each * j, g * G + each * (j + 1), sequence, 0)

            @pl.when(g > 0)
            def _():
                step(g - 1)

        attended(g)
        return carry

    lax.fori_loop(0, groups - 1, group, 0)
    g = groups - 1
    for j, step in enumerate(steps):
        lax.fori_loop(g * G + each * j, min(g * G + each * (j + 1), n - 1), sequence, 0)
        step(g - 1)
    vcopy(n - 1, (n - 1) % NV).wait()
    seen_from(s_v, vbuf, seen_v, n - 1, (n - 1) % NV, (n - 1) % 2)
    attended(g)
    for step in steps:
        step(g)


def solution(mesh):
    n_dev = mesh.shape["tp"]

    def step(x, k_cache, v_cache, gain_a, wq, wo, gain_m, w_gate, w_up, w_down):
        n, d = x.shape
        cache = k_cache.shape[1]
        half = HEAD // 2
        angle = np.float32(cache - 1) * np.float32(THETA) ** (-np.arange(half, dtype=np.float32) / np.float32(half))
        angle = angle.astype(np.float32).astype(np.float64)
        cos, sin = np.cos(angle).astype(np.float32), np.sin(angle).astype(np.float32)
        turn = np.stack([np.concatenate([cos, cos]), np.concatenate([-sin, sin])])
        cols, ff = d // n_dev, w_gate.shape[1]
        rows = cache * 2
        out = pl.pallas_call(
            functools.partial(layer, n_dev),
            out_shape=jax.ShapeDtypeStruct((n // G, G, d), BF16),
            in_specs=[pl.BlockSpec(memory_space=pl.ANY)] * 11,
            out_specs=pl.BlockSpec(memory_space=pl.ANY),
            scratch_shapes=[
                pltpu.VMEM((NK, rows, HEAD), BF16),
                pltpu.VMEM((NV, rows, HEAD), BF16),
                pltpu.VMEM((n // G, G, d), BF16),
                pltpu.VMEM((n // G, G, cols), BF16),
                pltpu.VMEM((d // HEAD, HEAD), BF16),
                pltpu.VMEM((d // HEAD, HEAD), BF16),
                pltpu.VMEM((2, HEAD), F32),
                pltpu.VMEM((d, 2 * HEAD), BF16),
                pltpu.VMEM((2 * HEAD, d), BF16),
                pltpu.VMEM((d, ff), BF16),
                pltpu.VMEM((d, ff), BF16),
                pltpu.VMEM((ff, d), BF16),
                pltpu.VMEM((n, 2 * HEAD), F32),
                pltpu.VMEM((2, 8, rows // 2), F32),
                pltpu.VMEM((n, 8, HEAD), F32),
                pltpu.VMEM((n_dev, G, cols), F32),
                pltpu.VMEM((n_dev, G, cols), BF16),
                pltpu.VMEM((n_dev, G, cols), BF16),
                pltpu.VMEM((G, cols), BF16),
                pltpu.VMEM((G, d), BF16),
                pltpu.VMEM((n_dev, G, cols), BF16),
                pltpu.VMEM((n_dev, G, cols), BF16),
                pltpu.VMEM((G, cols), BF16),
                pltpu.SemaphoreType.DMA((NK,)),
                pltpu.SemaphoreType.DMA((NV,)),
                pltpu.SemaphoreType.DMA((10,)),
                pltpu.SemaphoreType.DMA,
                pltpu.SemaphoreType.DMA((4, n_dev)),
                pltpu.SemaphoreType.DMA((4, n_dev)),
            ],
            compiler_params=pltpu.CompilerParams(vmem_limit_bytes=60 << 20, collective_id=0, has_side_effects=True),
        )(
            x.reshape(n // G, G, d),
            k_cache.reshape(n, rows, HEAD),
            v_cache.reshape(n, rows, HEAD),
            gain_a.reshape(-1, HEAD),
            wq,
            wo,
            gain_m.reshape(-1, HEAD),
            w_gate,
            w_up,
            w_down,
            jnp.asarray(turn),
        )
        return out.reshape(n, d)

    states, cache, columns, rows_of = P("dp", None), P("dp", None, "tp", None), P(None, "tp"), P("tp", None)
    return jax.shard_map(
        step,
        mesh=mesh,
        in_specs=(states, cache, cache, P(None), columns, rows_of, P(None), columns, columns, rows_of),
        out_specs=states,
        check_vma=False,
    )
```

time: 201 us -> 139 us (0.69)
  waiting for transfers between devices: 87.6 us -> 0 us
  Pallas kernels: 81.9 us -> 137 us
  between operations: 13.5 us -> 0.01 us
  matrix products: 12.3 us -> 0 us
  other arithmetic: 5.54 us -> 0 us
    psum x2 -> x0, waiting for transfers between devices: 87.5 us -> none  [added(): lax.psum(term.astype(jnp.bfloat16), 'tp').astype(jnp.float32)]
    pallas_call x1, Pallas kernels: 81.9 us -> 137 us  [step(): pl.pallas_call(functools.partial(layer, n_dev), out_shape=jax.ShapeDtypeS...]
    dot_general x4 -> x0, matrix products: 12.3 us -> none  [the longest x1 5.81 us: step(): jnp.dot(hidden_of(normed(h, gain_m), w_gate, w_up), w_down, preferred_ele...]
    convert_element_type x4 -> x0, other arithmetic: 3.13 us -> none  [the longest x1 1.71 us: added(): (t.astype(jnp.float32) + lax.psum(term.astype(jnp.bfloat16), 'tp').astype...]
    reduce_sum x2 -> x0, other arithmetic: 2.33 us -> none  [normed(): scale = lax.rsqrt(jnp.mean(wide * wide, -1, keepdims=True) + 1e-06)]
  transfers between devices with their start and end apart: 2 -> 0, of which waited for: 2 -> 0; matrix products, arithmetic and copies ran while one was open for 0% -> 0% of each run, Pallas kernels for 0% -> 0%
where the time goes in v2:
time: 139 us
  Pallas kernels  137 us (99%)
  local copies, waits for them, and re-layouts  1.67 us (1%)
    pallas_call x1, Pallas kernels, step(): pl.pallas_call(functools.partial(layer, n_dev), out_shape=jax.ShapeDtypeS...  137 us

profile of v2, /device:TPU:0, one launch (start us, length us, event | category | flops | bytes accessed | tf_op | source)
XLA Modules:
  0.0 138.6 jit_solution(1534357986275587117)
XLA Ops:
  0.0 136.9 %shard_map.109 = bf16[8,8,2048]{2,1,0:T(8,128)(2,1)} custom-call(bf16[8,8,2048]{2,1,0:T(8,128)(2,1)} %bitcast.7, bf16[64,8192,128]{2,1,0:T(8,128)(2,1)} %bitcast.1.k_ref, bf16[64,8192,128]{2,1,0:T(8,128)(2,1)} %bitcast.2.v_ref, bf16[16,128]{1,0:T(8,128)(2,1)} %bitcast.8, bf16[2048,256]{1,0:T(8,128)(2,1)} %wq_ref.1, bf16[256,2048]{1,0:T(8,128)(2,1)} %wo_ref.1, ...), custom_call_target="tpu_custom_call" | custom-call | tf_op jit(solution)/shard_map/pallas_call | solution.py:286
  136.9 1.7 %copy.13 = bf16[64,2048]{1,0:T(8,128)(2,1)} copy(bf16[64,2048]{1,0:T(8,128)(2,1)} %bitcast.6) | data formatting | bytes 524288

commit v3 on v2

--- a/solution.py
+++ b/solution.py
@@ -28,7 +28,7 @@
     return jnp.concatenate([t, t], 0).astype(BF16)
 
 
-def scores_of(q_ref, kbuf, s_ref, b, slot, par):
+def scores_of(q_ref, kbuf, s_ref, b, slot):
     row = q_ref[pl.ds(b, 1), :]
     q0 = jnp.broadcast_to(row[:, :HEAD], (16, HEAD))
     q1 = jnp.broadcast_to(row[:, HEAD:], (16, HEAD))
@@ -40,15 +40,15 @@
         ka = kbuf[slot, 512 * j : 512 * j + 256, :]
         kb = kbuf[slot, 512 * j + 256 : 512 * j + 512, :]
         s = lax.dot_general(lhs, jnp.concatenate([ka, kb], 1), (((1,), (1,)), ((), ())), preferred_element_type=F32)
-        s_ref[par, :, 256 * j : 256 * j + 256] = s[:8]
-
-
-def seen_from(s_ref, vbuf, seen_ref, b, slot, par):
-    tiles = vbuf.shape[1] // 512
+        s_ref[:, 256 * j : 256 * j + 256] = s[:8]
+
+
+def weights_of(s_ref, p_ref):
+    tiles = s_ref.shape[1] // 256
     r = lax.broadcasted_iota(jnp.int32, (8, 256), 0)
     c = lax.broadcasted_iota(jnp.int32, (8, 256), 1)
     mine = (r & 1) == (c & 1)
-    t = [jnp.where(mine, s_ref[par, :, 256 * j : 256 * j + 256], -1e30) for j in range(tiles)]
+    t = [jnp.where(mine, s_ref[:, 256 * j : 256 * j + 256], -1e30) for j in range(tiles)]
     m = functools.reduce(jnp.maximum, t)
     m = jnp.max(jnp.maximum(m[:, :128], m[:, 128:]), 1, keepdims=True)
     m = jnp.broadcast_to(m, (8, 128))
@@ -62,11 +62,16 @@
     l = l + pltpu.roll(l, 2, 0)
     inv = 1.0 / l
     inv = jnp.concatenate([inv, inv], 1)
+    for j in range(tiles):
+        p_ref[:, 256 * j : 256 * j + 256] = twice(p[j] * inv)
+
+
+def seen_from(p_ref, vbuf, seen_ref, b, slot):
     o = jnp.zeros((16, 256), F32)
-    for j in range(tiles):
+    for j in range(vbuf.shape[1] // 512):
         va = vbuf[slot, 512 * j : 512 * j + 256, :]
         vb = vbuf[slot, 512 * j + 256 : 512 * j + 512, :]
-        o = o + jnp.dot(twice(p[j] * inv), jnp.concatenate([va, vb], 1), preferred_element_type=F32)
+        o = o + jnp.dot(p_ref[:, 256 * j : 256 * j + 256], jnp.concatenate([va, vb], 1), preferred_element_type=F32)
     o = o[:8]
     seen_ref[b] = o[:, :128] + pltpu.roll(o[:, 128:], 6, 0)
 
@@ -74,7 +79,7 @@
 def layer(
     n_dev, x_ref, k_ref, v_ref, ga_ref, wq_ref, wo_ref, gm_ref, wg_ref, wu_ref, wd_ref, turn_ref, out_ref,
     kbuf, vbuf, x_v, xc_v, ga_v, gm_v, turn_v, wq_v, wo_v, wg_v, wu_v, wd_v,
-    q_v, s_v, seen_v, own_v, hsend, hrecv, hmine, hfull, ysend, yrecv, ymine,
+    q_v, s0_v, s1_v, p0_v, p1_v, seen_v, own_v, hsend, hrecv, hmine, hfull, ysend, yrecv, ymine,
     ksem, vsem, wsem, outsem, send_sem, recv_sem,
 ):
     me = lax.axis_index("tp")
@@ -222,49 +227,57 @@
     loads[5].wait()
     pl.semaphore_wait(barrier, n_dev - 1)
 
-    kcopy(0, 0).wait()
-    scores_of(q_v, kbuf, s_v, 0, 0, 0)
-    kcopy(NK, 0).start()
-
-    def sequence(i, carry):
-        kslot, vslot = lax.rem(i + 1, NK), lax.rem(i, NV)
-        kcopy(i + 1, kslot).wait()
-        vcopy(i, vslot).wait()
-        par = lax.rem(i, 2)
-        scores_of(q_v, kbuf, s_v, i + 1, kslot, 1 - par)
-        seen_from(s_v, vbuf, seen_v, i, vslot, par)
-
-        @pl.when(i + 1 + NK < n)
-        def _():
-            kcopy(i + 1 + NK, kslot).start()
+    score, weight = (s0_v, s1_v), (p0_v, p1_v)
+    for b in range(2):
+        kcopy(b, b).wait()
+        scores_of(q_v, kbuf, score[b], b, b)
+        kcopy(b + NK, b).start()
+
+    def pair(p, carry):
+        i = 2 * p
+        for b in range(2):
+            kcopy(i + b + 2, lax.rem(i + b + 2, NK)).wait()
+            vcopy(i + b, lax.rem(i + b, NV)).wait()
+        for b in range(2):
+            weights_of(score[b], weight[b])
+        for b in range(2):
+            scores_of(q_v, kbuf, score[b], i + b + 2, lax.rem(i + b + 2, NK))
+        for b in range(2):
+            seen_from(weight[b], vbuf, seen_v, i + b, lax.rem(i + b, NV))
+
+        @pl.when(i + 2 + NK < n)
+        def _():
+            for b in range(2):
+                kcopy(i + b + 2 + NK, lax.rem(i + b + 2, NK)).start()
 
         @pl.when(i + NV < n)
         def _():
-            vcopy(i + NV, vslot).start()
-
-        return carry
-
-    steps = (half, through, whole, done)
-    each = G // len(steps)
-
-    def group(g, carry):
-        for j, step in enumerate(steps):
-            lax.fori_loop(g * G + each * j, g * G + each * (j + 1), sequence, 0)
-
-            @pl.when(g > 0)
+            for b in range(2):
+                vcopy(i + b + NV, lax.rem(i + b, NV)).start()
+
+        g, j = p // pairs, lax.rem(p, pairs)
+        for at, step in enumerate(steps):
+
+            @pl.when((j == at) & (g > 0))
             def _():
                 step(g - 1)
 
-        attended(g)
+        @pl.when(j == pairs - 1)
+        def _():
+            attended(g)
+
         return carry
 
-    lax.fori_loop(0, groups - 1, group, 0)
+    steps = (half, through, whole, done)
+    pairs = G // 2
+    lax.fori_loop(0, n // 2 - 1, pair, 0)
+    for b in range(2):
+        weights_of(score[b], weight[b])
+    for b in range(n - 2, n):
+        vcopy(b, b % NV).wait()
+        seen_from(weight[b % 2], vbuf, seen_v, b, b % NV)
     g = groups - 1
-    for j, step in enumerate(steps):
-        lax.fori_loop(g * G + each * j, min(g * G + each * (j + 1), n - 1), sequence, 0)
-        step(g - 1)
-    vcopy(n - 1, (n - 1) % NV).wait()
-    seen_from(s_v, vbuf, seen_v, n - 1, (n - 1) % NV, (n - 1) % 2)
+    done(g - 1)
     attended(g)
     for step in steps:
         step(g)
@@ -302,7 +315,10 @@
                 pltpu.VMEM((d, ff), BF16),
                 pltpu.VMEM((ff, d), BF16),
                 pltpu.VMEM((n, 2 * HEAD), F32),
-                pltpu.VMEM((2, 8, rows // 2), F32),
+                pltpu.VMEM((8, rows // 2), F32),
+                pltpu.VMEM((8, rows // 2), F32),
+                pltpu.VMEM((16, rows // 2), BF16),
+                pltpu.VMEM((16, rows // 2), BF16),
                 pltpu.VMEM((n, 8, HEAD), F32),
                 pltpu.VMEM((n_dev, G, cols), F32),
                 pltpu.VMEM((n_dev, G, cols), BF16),

time: 139 us -> 139 us (level)
  no operation moved by 1% of the time
where the time goes in v3:
time: 139 us
  Pallas kernels  137 us (99%)
  local copies, waits for them, and re-layouts  1.67 us (1%)
    pallas_call x1, Pallas kernels, step(): pl.pallas_call(functools.partial(layer, n_dev), out_shape=jax.ShapeDtypeS...  137 us

profile of v3, /device:TPU:0, one launch (start us, length us, event | category | flops | bytes accessed | tf_op | source)
XLA Modules:
  0.0 139.0 jit_solution(1935473240921703834)
XLA Ops:
  0.0 137.4 %shard_map.109 = bf16[8,8,2048]{2,1,0:T(8,128)(2,1)} custom-call(bf16[8,8,2048]{2,1,0:T(8,128)(2,1)} %bitcast.7, bf16[64,8192,128]{2,1,0:T(8,128)(2,1)} %bitcast.1.k_ref, bf16[64,8192,128]{2,1,0:T(8,128)(2,1)} %bitcast.2.v_ref, bf16[16,128]{1,0:T(8,128)(2,1)} %bitcast.8, bf16[2048,256]{1,0:T(8,128)(2,1)} %wq_ref.1, bf16[256,2048]{1,0:T(8,128)(2,1)} %wo_ref.1, ...), custom_call_target="tpu_custom_call" | custom-call | tf_op jit(solution)/shard_map/pallas_call | solution.py:299
  137.4 1.7 %copy.13 = bf16[64,2048]{1,0:T(8,128)(2,1)} copy(bf16[64,2048]{1,0:T(8,128)(2,1)} %bitcast.6) | data formatting | bytes 524288

commit v4 on v3

v4 whole, which is shorter than its diff:
```python
import functools

import jax
import jax.numpy as jnp
import numpy as np
from jax import lax
from jax.experimental import pallas as pl
from jax.experimental.pallas import tpu as pltpu
from jax.sharding import PartitionSpec as P

HEAD = 128
THETA = 10000
F32, BF16 = jnp.float32, jnp.bfloat16
LOG2E = 1.4426950408889634
BLOCK = 8
NK = NV = 6
GROUPS = [
    (0, 16, 7, 11, 15),
    (16, 16, 15, 19, 23),
    (32, 16, 23, 27, 29),
    (48, 8, 27, 30, 34),
    (56, 4, 29, 33, 36),
    (60, 4, 32, 35, 37),
]


def normed(wide, gain):
    gain = gain.astype(F32)
    gain = jnp.concatenate([gain[c : c + 1] for c in range(gain.shape[0])], 1)
    scale = lax.rsqrt(jnp.mean(wide * wide, -1, keepdims=True) + 1e-6)
    return (wide * scale * gain).astype(BF16)


def twice(t):
    return jnp.concatenate([t, t], 0).astype(BF16)


def scores_of(q_ref, kbuf, s_ref, b, slot):
    row = q_ref[pl.ds(b, 1), :]
    q0 = jnp.broadcast_to(row[:, :HEAD], (16, HEAD))
    q1 = jnp.broadcast_to(row[:, HEAD:], (16, HEAD))
    r = lax.broadcasted_iota(jnp.int32, (16, HEAD), 0)
    q = jnp.where((r & 1) == 0, q0, q1)
    first = (r & 2) == 0
    lhs = jnp.concatenate([jnp.where(first, q, 0.0), jnp.where(first, 0.0, q)], 1).astype(BF16)
    for j in range(kbuf.shape[1] // 512):
        ka = kbuf[slot, 512 * j : 512 * j + 256, :]
        kb = kbuf[slot, 512 * j + 256 : 512 * j + 512, :]
        s = lax.dot_general(lhs, jnp.concatenate([ka, kb], 1), (((1,), (1,)), ((), ())), preferred_element_type=F32)
        s_ref[:, 256 * j : 256 * j + 256] = s[:8]


def weights_of(s_ref, p_ref):
    tiles = s_ref.shape[1] // 256
    r = lax.broadcasted_iota(jnp.int32, (8, 256), 0)
    c = lax.broadcasted_iota(jnp.int32, (8, 256), 1)
    mine = (r & 1) == (c & 1)
    t = [jnp.where(mine, s_ref[:, 256 * j : 256 * j + 256], -1e30) for j in range(tiles)]
    m = functools.reduce(jnp.maximum, t)
    m = jnp.max(jnp.maximum(m[:, :128], m[:, 128:]), 1, keepdims=True)
    m = jnp.broadcast_to(m, (8, 128))
    m = jnp.maximum(m, pltpu.roll(m, 2, 0))
    m = jnp.concatenate([m, m], 1)
    k = HEAD**-0.5 * LOG2E
    p = [jnp.exp2((x - m) * k) for x in t]
    l = functools.reduce(jnp.add, p)
    l = jnp.sum(l[:, :128] + l[:, 128:], 1, keepdims=True)
    l = jnp.broadcast_to(l, (8, 128))
    l = l + pltpu.roll(l, 2, 0)
    inv = 1.0 / l
    inv = jnp.concatenate([inv, inv], 1)
    for j in range(tiles):
        p_ref[:, 256 * j : 256 * j + 256] = twice(p[j] * inv)


def seen_from(p_ref, vbuf, seen_ref, b, slot):
    o = jnp.zeros((16, 256), F32)
    for j in range(vbuf.shape[1] // 512):
        va = vbuf[slot, 512 * j : 512 * j + 256, :]
        vb = vbuf[slot, 512 * j + 256 : 512 * j + 512, :]
        o = o + jnp.dot(p_ref[:, 256 * j : 256 * j + 256], jnp.concatenate([va, vb], 1), preferred_element_type=F32)
    o = o[:8]
    seen_ref[b] = o[:, :128] + pltpu.roll(o[:, 128:], 6, 0)


def layer(
    n_dev, x_ref, k_ref, v_ref, ga_ref, wq_ref, wo_ref, gm_ref, wg_ref, wu_ref, wd_ref, turn_ref, out_ref,
    kbuf, vbuf, x_v, ga_v, gm_v, turn_v, wq_v, wo_v, wg_v, wu_v, wd_v,
    q_v, s0_v, s1_v, p0_v, p1_v, seen_v, y_v, *rest,
):
    n_groups = len(GROUPS)
    h_v, hterm, yterm = rest[:n_groups], rest[n_groups : 2 * n_groups], rest[2 * n_groups : 3 * n_groups]
    ksem, vsem, wsem, outsem, send_sem, recv_sem = rest[3 * n_groups :]
    me = lax.axis_index("tp")
    n = k_ref.shape[0]
    block = x_ref.shape[1]
    peers = [lax.rem(me + j, n_dev) for j in range(1, n_dev)]

    barrier = pltpu.get_barrier_semaphore()
    for peer in peers:
        pl.semaphore_signal(barrier, inc=1, device_id={"tp": peer}, device_id_type=pl.DeviceIdType.MESH)

    loads = [
        pltpu.make_async_copy(src, dst, wsem.at[i])
        for i, (src, dst) in enumerate(
            [
                (x_ref, x_v),
                (ga_ref, ga_v),
                (turn_ref, turn_v),
                (wq_ref, wq_v),
                (gm_ref, gm_v),
                (wo_ref, wo_v),
                (wg_ref, wg_v),
                (wu_ref, wu_v),
                (wd_ref, wd_v),
            ]
        )
    ]

    def kcopy(b, slot):
        return pltpu.make_async_copy(k_ref.at[b], kbuf.at[slot], ksem.at[slot])

    def vcopy(b, slot):
        return pltpu.make_async_copy(v_ref.at[b], vbuf.at[slot], vsem.at[slot])

    def rows_of(ref, g):
        first, count = GROUPS[g][:2]
        if count >= block:
            return jnp.concatenate([ref[b] for b in range(first // block, (first + count) // block)], 0)
        return ref[first // block, first % block : first % block + count, :]

    def exchange(g, phase, terms, peer, source):
        return pltpu.make_async_remote_copy(
            src_ref=terms.at[source],
            dst_ref=terms.at[source],
            send_sem=send_sem.at[g, phase, peer],
            recv_sem=recv_sem.at[g, phase, source],
            device_id={"tp": peer},
            device_id_type=pl.DeviceIdType.MESH,
        )

    def send(g, phase, terms, out):
        terms[me] = out[: GROUPS[g][1]].astype(BF16)
        for peer in peers:
            exchange(g, phase, terms, peer, me).start()

    def summed(g, phase, terms):
        for source in peers:
            exchange(g, phase, terms, me, source).wait_recv()
        for peer in peers:
            exchange(g, phase, terms, peer, me).wait_send()
        return functools.reduce(jnp.add, [terms[i].astype(F32) for i in range(n_dev)])

    def filled(t):
        return jnp.concatenate([t] * (16 // t.shape[0]), 0).astype(BF16)

    def attended(g):
        if g == 0:
            loads[5].wait()
        first, count = GROUPS[g][:2]
        seen = jnp.concatenate([seen_v[first : first + count, 0, :], seen_v[first : first + count, 1, :]], 1)
        send(g, 0, hterm[g], jnp.dot(filled(seen), wo_v[...], preferred_element_type=F32))

    def through(g):
        if g == 0:
            for load in (loads[4], *loads[6:]):
                load.wait()
        h = (rows_of(x_v, g).astype(F32) + summed(g, 0, hterm[g])).astype(BF16)
        h_v[g][...] = h
        b = filled(normed(h.astype(F32), gm_v[...]).astype(F32))
        gate = jnp.dot(b, wg_v[...], preferred_element_type=F32)
        up = jnp.dot(b, wu_v[...], preferred_element_type=F32)
        send(g, 1, yterm[g], jnp.dot((jax.nn.silu(gate) * up).astype(BF16), wd_v[...], preferred_element_type=F32))

    def out_copy(b):
        return pltpu.make_async_copy(y_v.at[b], out_ref.at[b], outsem.at[b])

    def done(g):
        first, count = GROUPS[g][:2]
        y = (h_v[g][...].astype(F32) + summed(g, 1, yterm[g])).astype(BF16)
        if count >= block:
            for b in range(count // block):
                y_v[first // block + b] = y[b * block : (b + 1) * block]
        else:
            y_v[first // block, first % block : first % block + count, :] = y
        if (first + count) % block == 0:
            for b in range(first // block, (first + count) // block):
                out_copy(b).start()

    for load in loads[:4]:
        load.start()
    for s in range(NK):
        kcopy(s, s).start()
        vcopy(s, s).start()
    for load in loads[4:]:
        load.start()

    for load in loads[:4]:
        load.wait()
    wide = jnp.concatenate([x_v[b] for b in range(n // block)], 0).astype(F32)
    q = jnp.dot(normed(wide, ga_v[...]), wq_v[...], preferred_element_type=F32).astype(BF16).astype(F32)
    for i in range(2):
        t = q[:, HEAD * i : HEAD * (i + 1)]
        t = t * turn_v[0:1, :] + pltpu.roll(t, HEAD // 2, 1) * turn_v[1:2, :]
        q_v[:, HEAD * i : HEAD * (i + 1)] = t.astype(BF16).astype(F32)
    pl.semaphore_wait(barrier, n_dev - 1)

    score, weight = (s0_v, s1_v), (p0_v, p1_v)
    for b in range(2):
        kcopy(b, b).wait()
        scores_of(q_v, kbuf, score[b], b, b)
        kcopy(b + NK, b).start()

    steps = sorted((at, order, step, g) for g in range(n_groups) for order, (step, at) in enumerate(zip((attended, through, done), GROUPS[g][2:])))

    def pair(p, carry):
        i = 2 * p
        for b in range(2):
            kcopy(i + b + 2, lax.rem(i + b + 2, NK)).wait()
            vcopy(i + b, lax.rem(i + b, NV)).wait()
        for b in range(2):
            weights_of(score[b], weight[b])
        for b in range(2):
            scores_of(q_v, kbuf, score[b], i + b + 2, lax.rem(i + b + 2, NK))
        for b in range(2):
            seen_from(weight[b], vbuf, seen_v, i + b, lax.rem(i + b, NV))

        @pl.when(i + 2 + NK < n)
        def _():
            for b in range(2):
                kcopy(i + b + 2 + NK, lax.rem(i + b + 2, NK)).start()

        @pl.when(i + NV < n)
        def _():
            for b in range(2):
                vcopy(i + b + NV, lax.rem(i + b, NV)).start()

        for at, _, step, g in steps:
            if at < n // 2 - 1:

                @pl.when(p == at)
                def _():
                    step(g)

        return carry

    lax.fori_loop(0, n // 2 - 1, pair, 0)
    for b in range(2):
        weights_of(score[b], weight[b])
    for b in range(n - 2, n):
        vcopy(b, b % NV).wait()
        seen_from(weight[b % 2], vbuf, seen_v, b, b % NV)
    for at, _, step, g in steps:
        if at >= n // 2 - 1:
            step(g)
    for b in range(n // block):
        out_copy(b).wait()


def solution(mesh):
    n_dev = mesh.shape["tp"]

    def step(x, k_cache, v_cache, gain_a, wq, wo, gain_m, w_gate, w_up, w_down):
        n, d = x.shape
        cache = k_cache.shape[1]
        half = HEAD // 2
        angle = np.float32(cache - 1) * np.float32(THETA) ** (-np.arange(half, dtype=np.float32) / np.float32(half))
        angle = angle.astype(np.float32).astype(np.float64)
        cos, sin = np.cos(angle).astype(np.float32), np.sin(angle).astype(np.float32)
        turn = np.stack([np.concatenate([cos, cos]), np.concatenate([-sin, sin])])
        ff = w_gate.shape[1]
        rows = cache * 2
        out = pl.pallas_call(
            functools.partial(layer, n_dev),
            out_shape=jax.ShapeDtypeStruct((n // BLOCK, BLOCK, d), BF16),
            in_specs=[pl.BlockSpec(memory_space=pl.ANY)] * 11,
            out_specs=pl.BlockSpec(memory_space=pl.ANY),
            scratch_shapes=[
                pltpu.VMEM((NK, rows, HEAD), BF16),
                pltpu.VMEM((NV, rows, HEAD), BF16),
                pltpu.VMEM((n // BLOCK, BLOCK, d), BF16),
                pltpu.VMEM((d // HEAD, HEAD), BF16),
                pltpu.VMEM((d // HEAD, HEAD), BF16),
                pltpu.VMEM((2, HEAD), F32),
                pltpu.VMEM((d, 2 * HEAD), BF16),
                pltpu.VMEM((2 * HEAD, d), BF16),
                pltpu.VMEM((d, ff), BF16),
                pltpu.VMEM((d, ff), BF16),
                pltpu.VMEM((ff, d), BF16),
                pltpu.VMEM((n, 2 * HEAD), F32),
                pltpu.VMEM((8, rows // 2), F32),
                pltpu.VMEM((8, rows // 2), F32),
                pltpu.VMEM((16, rows // 2), BF16),
                pltpu.VMEM((16, rows // 2), BF16),
                pltpu.VMEM((n, 8, HEAD), F32),
                pltpu.VMEM((n // BLOCK, BLOCK, d), BF16),
                *[pltpu.VMEM((g[1], d), BF16) for g in GROUPS],
                *[pltpu.VMEM((n_dev, g[1], d), BF16) for g in GROUPS],
                *[pltpu.VMEM((n_dev, g[1], d), BF16) for g in GROUPS],
                pltpu.SemaphoreType.DMA((NK,)),
                pltpu.SemaphoreType.DMA((NV,)),
                pltpu.SemaphoreType.DMA((9,)),
                pltpu.SemaphoreType.DMA((n // BLOCK,)),
                pltpu.SemaphoreType.DMA((len(GROUPS), 2, n_dev)),
                pltpu.SemaphoreType.DMA((len(GROUPS), 2, n_dev)),
            ],
            compiler_params=pltpu.CompilerParams(vmem_limit_bytes=60 << 20, collective_id=0, has_side_effects=True),
        )(
            x.reshape(n // BLOCK, BLOCK, d),
            k_cache.reshape(n, rows, HEAD),
            v_cache.reshape(n, rows, HEAD),
            gain_a.reshape(-1, HEAD),
            wq,
            wo,
            gain_m.reshape(-1, HEAD),
            w_gate,
            w_up,
            w_down,
            jnp.asarray(turn),
        )
        return out.reshape(n, d)

    states, cache, columns, rows_of = P("dp", None), P("dp", None, "tp", None), P(None, "tp"), P("tp", None)
    return jax.shard_map(
        step,
        mesh=mesh,
        in_specs=(states, cache, cache, P(None), columns, rows_of, P(None), columns, columns, rows_of),
        out_specs=states,
        check_vma=False,
    )
```

time: 139 us -> 109 us (0.78)
  Pallas kernels: 137 us -> 107 us
    pallas_call x1, Pallas kernels: 137 us -> 107 us  [step(): pl.pallas_call(functools.partial(layer, n_dev), out_shape=jax.ShapeDtypeS...]
where the time goes in v4:
time: 109 us
  Pallas kernels  107 us (98%)
  local copies, waits for them, and re-layouts  1.67 us (2%)
    pallas_call x1, Pallas kernels, step(): pl.pallas_call(functools.partial(layer, n_dev), out_shape=jax.ShapeDtypeS...  107 us

profile of v4, /device:TPU:0, one launch (start us, length us, event | category | flops | bytes accessed | tf_op | source)
XLA Modules:
  0.0 109.0 jit_solution(7318705607020167309)
XLA Ops:
  0.0 107.3 %shard_map.109 = bf16[8,8,2048]{2,1,0:T(8,128)(2,1)} custom-call(bf16[8,8,2048]{2,1,0:T(8,128)(2,1)} %bitcast.7, bf16[64,8192,128]{2,1,0:T(8,128)(2,1)} %bitcast.1.k_ref, bf16[64,8192,128]{2,1,0:T(8,128)(2,1)} %bitcast.2.v_ref, bf16[16,128]{1,0:T(8,128)(2,1)} %bitcast.8, bf16[2048,256]{1,0:T(8,128)(2,1)} %wq_ref.1, bf16[256,2048]{1,0:T(8,128)(2,1)} %wo_ref.1, ...), custom_call_target="tpu_custom_call" | custom-call | tf_op jit(solution)/shard_map/pallas_call | solution.py:273
  107.3 1.7 %copy.13 = bf16[64,2048]{1,0:T(8,128)(2,1)} copy(bf16[64,2048]{1,0:T(8,128)(2,1)} %bitcast.6) | data formatting | bytes 524288

commit v5 on v4

--- a/solution.py
+++ b/solution.py
@@ -13,15 +13,19 @@
 F32, BF16 = jnp.float32, jnp.bfloat16
 LOG2E = 1.4426950408889634
 BLOCK = 8
-NK = NV = 6
-GROUPS = [
-    (0, 16, 7, 11, 15),
-    (16, 16, 15, 19, 23),
-    (32, 16, 23, 27, 29),
-    (48, 8, 27, 30, 34),
-    (56, 4, 29, 33, 36),
-    (60, 4, 32, 35, 37),
-]
+NK = NV = 8
+GROUPS = [(0, 16), (16, 16), (32, 16), (48, 8), (56, 4), (60, 4)]
+STREAM = {
+    7: [("attended", 0)],
+    11: [("through", 0)],
+    15: [("attended", 1), ("done", 0)],
+    19: [("through", 1)],
+    23: [("attended", 2), ("done", 1)],
+    26: [("through", 2)],
+    27: [("attended", 3)],
+    29: [("attended", 4)],
+}
+TAIL = [("attended", 5), ("through", 3, 4), ("done", 2), ("through", 5), ("done", 3), ("done", 4), ("done", 5)]
 
 
 def normed(wide, gain):
@@ -86,11 +90,11 @@
 def layer(
     n_dev, x_ref, k_ref, v_ref, ga_ref, wq_ref, wo_ref, gm_ref, wg_ref, wu_ref, wd_ref, turn_ref, out_ref,
     kbuf, vbuf, x_v, ga_v, gm_v, turn_v, wq_v, wo_v, wg_v, wu_v, wd_v,
-    q_v, s0_v, s1_v, p0_v, p1_v, seen_v, y_v, *rest,
+    q_v, s0_v, s1_v, p0_v, p1_v, seen_v, *rest,
 ):
     n_groups = len(GROUPS)
     h_v, hterm, yterm = rest[:n_groups], rest[n_groups : 2 * n_groups], rest[2 * n_groups : 3 * n_groups]
-    ksem, vsem, wsem, outsem, send_sem, recv_sem = rest[3 * n_groups :]
+    ksem, vsem, wsem, send_sem, recv_sem = rest[3 * n_groups :]
     me = lax.axis_index("tp")
     n = k_ref.shape[0]
     block = x_ref.shape[1]
@@ -124,7 +128,7 @@
         return pltpu.make_async_copy(v_ref.at[b], vbuf.at[slot], vsem.at[slot])
 
     def rows_of(ref, g):
-        first, count = GROUPS[g][:2]
+        first, count = GROUPS[g]
         if count >= block:
             return jnp.concatenate([ref[b] for b in range(first // block, (first + count) // block)], 0)
         return ref[first // block, first % block : first % block + count, :]
@@ -151,41 +155,48 @@
             exchange(g, phase, terms, peer, me).wait_send()
         return functools.reduce(jnp.add, [terms[i].astype(F32) for i in range(n_dev)])
 
-    def filled(t):
-        return jnp.concatenate([t] * (16 // t.shape[0]), 0).astype(BF16)
+    def filled(*parts):
+        parts = list(parts)
+        while sum(t.shape[0] for t in parts) < 16:
+            parts.append(parts[-1])
+        return jnp.concatenate(parts, 0).astype(BF16)
 
     def attended(g):
         if g == 0:
             loads[5].wait()
-        first, count = GROUPS[g][:2]
+        first, count = GROUPS[g]
         seen = jnp.concatenate([seen_v[first : first + count, 0, :], seen_v[first : first + count, 1, :]], 1)
         send(g, 0, hterm[g], jnp.dot(filled(seen), wo_v[...], preferred_element_type=F32))
 
-    def through(g):
-        if g == 0:
+    def through(*gs):
+        if 0 in gs:
             for load in (loads[4], *loads[6:]):
                 load.wait()
-        h = (rows_of(x_v, g).astype(F32) + summed(g, 0, hterm[g])).astype(BF16)
-        h_v[g][...] = h
-        b = filled(normed(h.astype(F32), gm_v[...]).astype(F32))
+        b = []
+        for g in gs:
+            h = (rows_of(x_v, g).astype(F32) + summed(g, 0, hterm[g])).astype(BF16)
+            h_v[g][...] = h
+            b.append(normed(h.astype(F32), gm_v[...]).astype(F32))
+        b = filled(*b)
         gate = jnp.dot(b, wg_v[...], preferred_element_type=F32)
         up = jnp.dot(b, wu_v[...], preferred_element_type=F32)
-        send(g, 1, yterm[g], jnp.dot((jax.nn.silu(gate) * up).astype(BF16), wd_v[...], preferred_element_type=F32))
-
-    def out_copy(b):
-        return pltpu.make_async_copy(y_v.at[b], out_ref.at[b], outsem.at[b])
+        out = jnp.dot((jax.nn.silu(gate) * up).astype(BF16), wd_v[...], preferred_element_type=F32)
+        at = 0
+        for g in gs:
+            count = GROUPS[g][1]
+            send(g, 1, yterm[g], out[at : at + count])
+            at += count
 
     def done(g):
-        first, count = GROUPS[g][:2]
+        first, count = GROUPS[g]
         y = (h_v[g][...].astype(F32) + summed(g, 1, yterm[g])).astype(BF16)
         if count >= block:
             for b in range(count // block):
-                y_v[first // block + b] = y[b * block : (b + 1) * block]
+                out_ref[first // block + b] = y[b * block : (b + 1) * block]
         else:
-            y_v[first // block, first % block : first % block + count, :] = y
-        if (first + count) % block == 0:
-            for b in range(first // block, (first + count) // block):
-                out_copy(b).start()
+            out_ref[first // block, first % block : first % block + count, :] = y
+
+    named = {"attended": attended, "through": through, "done": done}
 
     for load in loads[:4]:
         load.start()
@@ -210,8 +221,6 @@
         kcopy(b, b).wait()
         scores_of(q_v, kbuf, score[b], b, b)
         kcopy(b + NK, b).start()
-
-    steps = sorted((at, order, step, g) for g in range(n_groups) for order, (step, at) in enumerate(zip((attended, through, done), GROUPS[g][2:])))
 
     def pair(p, carry):
         i = 2 * p
@@ -235,26 +244,33 @@
             for b in range(2):
                 vcopy(i + b + NV, lax.rem(i + b, NV)).start()
 
-        for at, _, step, g in steps:
-            if at < n // 2 - 1:
-
-                @pl.when(p == at)
-                def _():
-                    step(g)
+        for at, steps in STREAM.items():
+
+            @pl.when(p == at)
+            def _():
+                for step, *gs in steps:
+                    named[step](*gs)
 
         return carry
 
-    lax.fori_loop(0, n // 2 - 1, pair, 0)
+    lax.fori_loop(0, n // 2 - 2, pair, 0)
+    for b in range(2):
+        kcopy(n - 2 + b, (n - 2 + b) % NK).wait()
     for b in range(2):
         weights_of(score[b], weight[b])
-    for b in range(n - 2, n):
-        vcopy(b, b % NV).wait()
-        seen_from(weight[b % 2], vbuf, seen_v, b, b % NV)
-    for at, _, step, g in steps:
-        if at >= n // 2 - 1:
-            step(g)
-    for b in range(n // block):
-        out_copy(b).wait()
+    for b in range(2):
+        scores_of(q_v, kbuf, score[b], n - 2 + b, (n - 2 + b) % NK)
+    for b in range(2):
+        vcopy(n - 4 + b, (n - 4 + b) % NV).wait()
+    for b in range(2):
+        seen_from(weight[b], vbuf, seen_v, n - 4 + b, (n - 4 + b) % NV)
+    for b in range(2):
+        weights_of(score[b], weight[b])
+    for b in range(2):
+        vcopy(n - 2 + b, (n - 2 + b) % NV).wait()
+        seen_from(weight[b], vbuf, seen_v, n - 2 + b, (n - 2 + b) % NV)
+    for step, *gs in TAIL:
+        named[step](*gs)
 
 
 def solution(mesh):
@@ -274,7 +290,7 @@
             functools.partial(layer, n_dev),
             out_shape=jax.ShapeDtypeStruct((n // BLOCK, BLOCK, d), BF16),
             in_specs=[pl.BlockSpec(memory_space=pl.ANY)] * 11,
-            out_specs=pl.BlockSpec(memory_space=pl.ANY),
+            out_specs=pl.BlockSpec(memory_space=pltpu.VMEM),
             scratch_shapes=[
                 pltpu.VMEM((NK, rows, HEAD), BF16),
                 pltpu.VMEM((NV, rows, HEAD), BF16),
@@ -293,18 +309,16 @@
                 pltpu.VMEM((16, rows // 2), BF16),
                 pltpu.VMEM((16, rows // 2), BF16),
                 pltpu.VMEM((n, 8, HEAD), F32),
-                pltpu.VMEM((n // BLOCK, BLOCK, d), BF16),
                 *[pltpu.VMEM((g[1], d), BF16) for g in GROUPS],
                 *[pltpu.VMEM((n_dev, g[1], d), BF16) for g in GROUPS],
                 *[pltpu.VMEM((n_dev, g[1], d), BF16) for g in GROUPS],
                 pltpu.SemaphoreType.DMA((NK,)),
                 pltpu.SemaphoreType.DMA((NV,)),
                 pltpu.SemaphoreType.DMA((9,)),
-                pltpu.SemaphoreType.DMA((n // BLOCK,)),
                 pltpu.SemaphoreType.DMA((len(GROUPS), 2, n_dev)),
                 pltpu.SemaphoreType.DMA((len(GROUPS), 2, n_dev)),
             ],
-            compiler_params=pltpu.CompilerParams(vmem_limit_bytes=60 << 20, collective_id=0, has_side_effects=True),
+            compiler_params=pltpu.CompilerParams(vmem_limit_bytes=56 << 20, collective_id=0, has_side_effects=True),
         )(
             x.reshape(n // BLOCK, BLOCK, d),
             k_cache.reshape(n, rows, HEAD),

time: 109 us -> 104 us (0.954)
  Pallas kernels: 107 us -> 103 us
    pallas_call x1, Pallas kernels: 107 us -> 103 us  [step(): pl.pallas_call(functools.partial(layer, n_dev), out_shape=jax.ShapeDtypeS...]
where the time goes in v5:
time: 104 us
  Pallas kernels  103 us (99%)
  local copies, waits for them, and re-layouts  1.67 us (2%)
    pallas_call x1, Pallas kernels, step(): pl.pallas_call(functools.partial(layer, n_dev), out_shape=jax.ShapeDtypeS...  103 us

profile of v5, /device:TPU:0, one launch (start us, length us, event | category | flops | bytes accessed | tf_op | source)
XLA Modules:
  0.0 104.2 jit_solution(13605087192882931953)
XLA Ops:
  0.0 102.5 %shard_map.109 = bf16[8,8,2048]{2,1,0:T(8,128)(2,1)} custom-call(bf16[8,8,2048]{2,1,0:T(8,128)(2,1)} %bitcast.7, bf16[64,8192,128]{2,1,0:T(8,128)(2,1)} %bitcast.1.k_ref, bf16[64,8192,128]{2,1,0:T(8,128)(2,1)} %bitcast.2.v_ref, bf16[16,128]{1,0:T(8,128)(2,1)} %bitcast.8, bf16[2048,256]{1,0:T(8,128)(2,1)} %wq_ref.1, bf16[256,2048]{1,0:T(8,128)(2,1)} %wo_ref.1, ...), custom_call_target="tpu_custom_call" | custom-call | tf_op jit(solution)/shard_map/pallas_call | solution.py:289
  102.5 1.7 %copy.13 = bf16[64,2048]{1,0:T(8,128)(2,1)} copy(bf16[64,2048]{1,0:T(8,128)(2,1)} %bitcast.6) | data formatting | bytes 524288

commit v6 on v5

--- a/solution.py
+++ b/solution.py
@@ -14,7 +14,8 @@
 LOG2E = 1.4426950408889634
 BLOCK = 8
 NK = NV = 8
-GROUPS = [(0, 16), (16, 16), (32, 16), (48, 8), (56, 4), (60, 4)]
+GROUPS = [(0, 16), (16, 16), (32, 16), (48, 8), (56, 4), (60, 2), (62, 2)]
+JOINED = [(0,), (1,), (2,), (3,), (4, 5, 6)]
 STREAM = {
     7: [("attended", 0)],
     11: [("through", 0)],
@@ -25,7 +26,12 @@
     27: [("attended", 3)],
     29: [("attended", 4)],
 }
-TAIL = [("attended", 5), ("through", 3, 4), ("done", 2), ("through", 5), ("done", 3), ("done", 4), ("done", 5)]
+LATE = [("attended", 5)]
+TAIL = [("attended", 6), ("through", 3), ("done", 2), ("through", 4), ("done", 3), ("done", 4)]
+
+
+def rows_in(m):
+    return GROUPS[JOINED[m][0]][0], sum(GROUPS[g][1] for g in JOINED[m])
 
 
 def normed(wide, gain):
@@ -92,17 +98,13 @@
     kbuf, vbuf, x_v, ga_v, gm_v, turn_v, wq_v, wo_v, wg_v, wu_v, wd_v,
     q_v, s0_v, s1_v, p0_v, p1_v, seen_v, *rest,
 ):
-    n_groups = len(GROUPS)
-    h_v, hterm, yterm = rest[:n_groups], rest[n_groups : 2 * n_groups], rest[2 * n_groups : 3 * n_groups]
-    ksem, vsem, wsem, send_sem, recv_sem = rest[3 * n_groups :]
+    a, m = len(GROUPS), len(JOINED)
+    h_v, hterm, yterm = rest[:m], rest[m : m + a], rest[m + a : 2 * m + a]
+    ksem, vsem, wsem, send_sem, recv_sem = rest[2 * m + a :]
     me = lax.axis_index("tp")
     n = k_ref.shape[0]
     block = x_ref.shape[1]
     peers = [lax.rem(me + j, n_dev) for j in range(1, n_dev)]
-
-    barrier = pltpu.get_barrier_semaphore()
-    for peer in peers:
-        pl.semaphore_signal(barrier, inc=1, device_id={"tp": peer}, device_id_type=pl.DeviceIdType.MESH)
 
     loads = [
         pltpu.make_async_copy(src, dst, wsem.at[i])
@@ -127,32 +129,31 @@
     def vcopy(b, slot):
         return pltpu.make_async_copy(v_ref.at[b], vbuf.at[slot], vsem.at[slot])
 
-    def rows_of(ref, g):
-        first, count = GROUPS[g]
+    def rows_of(ref, first, count):
         if count >= block:
             return jnp.concatenate([ref[b] for b in range(first // block, (first + count) // block)], 0)
         return ref[first // block, first % block : first % block + count, :]
 
-    def exchange(g, phase, terms, peer, source):
+    def exchange(at, terms, peer, source):
         return pltpu.make_async_remote_copy(
             src_ref=terms.at[source],
             dst_ref=terms.at[source],
-            send_sem=send_sem.at[g, phase, peer],
-            recv_sem=recv_sem.at[g, phase, source],
+            send_sem=send_sem.at[at, peer],
+            recv_sem=recv_sem.at[at, source],
             device_id={"tp": peer},
             device_id_type=pl.DeviceIdType.MESH,
         )
 
-    def send(g, phase, terms, out):
-        terms[me] = out[: GROUPS[g][1]].astype(BF16)
+    def send(at, terms, out):
+        terms[me] = out[: terms.shape[1]].astype(BF16)
         for peer in peers:
-            exchange(g, phase, terms, peer, me).start()
-
-    def summed(g, phase, terms):
+            exchange(at, terms, peer, me).start()
+
+    def summed(at, terms):
         for source in peers:
-            exchange(g, phase, terms, me, source).wait_recv()
+            exchange(at, terms, me, source).wait_recv()
         for peer in peers:
-            exchange(g, phase, terms, peer, me).wait_send()
+            exchange(at, terms, peer, me).wait_send()
         return functools.reduce(jnp.add, [terms[i].astype(F32) for i in range(n_dev)])
 
     def filled(*parts):
@@ -166,37 +167,34 @@
             loads[5].wait()
         first, count = GROUPS[g]
         seen = jnp.concatenate([seen_v[first : first + count, 0, :], seen_v[first : first + count, 1, :]], 1)
-        send(g, 0, hterm[g], jnp.dot(filled(seen), wo_v[...], preferred_element_type=F32))
-
-    def through(*gs):
-        if 0 in gs:
+        send(g, hterm[g], jnp.dot(filled(seen), wo_v[...], preferred_element_type=F32))
+
+    def through(m):
+        if m == 0:
             for load in (loads[4], *loads[6:]):
                 load.wait()
-        b = []
-        for g in gs:
-            h = (rows_of(x_v, g).astype(F32) + summed(g, 0, hterm[g])).astype(BF16)
-            h_v[g][...] = h
-            b.append(normed(h.astype(F32), gm_v[...]).astype(F32))
-        b = filled(*b)
+        parts, at = [], 0
+        for g in JOINED[m]:
+            first, count = GROUPS[g]
+            h = (rows_of(x_v, first, count).astype(F32) + summed(g, hterm[g])).astype(BF16)
+            h_v[m][at : at + count, :] = h
+            at += count
+            parts.append(normed(h.astype(F32), gm_v[...]).astype(F32))
+        b = filled(jnp.concatenate(parts, 0))
         gate = jnp.dot(b, wg_v[...], preferred_element_type=F32)
         up = jnp.dot(b, wu_v[...], preferred_element_type=F32)
         out = jnp.dot((jax.nn.silu(gate) * up).astype(BF16), wd_v[...], preferred_element_type=F32)
-        at = 0
-        for g in gs:
-            count = GROUPS[g][1]
-            send(g, 1, yterm[g], out[at : at + count])
-            at += count
-
-    def done(g):
-        first, count = GROUPS[g]
-        y = (h_v[g][...].astype(F32) + summed(g, 1, yterm[g])).astype(BF16)
-        if count >= block:
-            for b in range(count // block):
-                out_ref[first // block + b] = y[b * block : (b + 1) * block]
-        else:
-            out_ref[first // block, first % block : first % block + count, :] = y
-
-    named = {"attended": attended, "through": through, "done": done}
+        send(len(GROUPS) + m, yterm[m], out)
+
+    def done(m):
+        first, count = rows_in(m)
+        y = (h_v[m][...].astype(F32) + summed(len(GROUPS) + m, yterm[m])).astype(BF16)
+        for b in range(count // block):
+            out_ref[first // block + b] = y[b * block : (b + 1) * block]
+
+    def run(steps):
+        for step, which in steps:
+            {"attended": attended, "through": through, "done": done}[step](which)
 
     for load in loads[:4]:
         load.start()
@@ -205,6 +203,9 @@
         vcopy(s, s).start()
     for load in loads[4:]:
         load.start()
+    barrier = pltpu.get_barrier_semaphore()
+    for peer in peers:
+        pl.semaphore_signal(barrier, inc=1, device_id={"tp": peer}, device_id_type=pl.DeviceIdType.MESH)
 
     for load in loads[:4]:
         load.wait()
@@ -248,8 +249,7 @@
 
             @pl.when(p == at)
             def _():
-                for step, *gs in steps:
-                    named[step](*gs)
+                run(steps)
 
         return carry
 
@@ -266,11 +266,11 @@
         seen_from(weight[b], vbuf, seen_v, n - 4 + b, (n - 4 + b) % NV)
     for b in range(2):
         weights_of(score[b], weight[b])
+    run(LATE)
     for b in range(2):
         vcopy(n - 2 + b, (n - 2 + b) % NV).wait()
         seen_from(weight[b], vbuf, seen_v, n - 2 + b, (n - 2 + b) % NV)
-    for step, *gs in TAIL:
-        named[step](*gs)
+    run(TAIL)
 
 
 def solution(mesh):
@@ -309,14 +309,14 @@
                 pltpu.VMEM((16, rows // 2), BF16),
                 pltpu.VMEM((16, rows // 2), BF16),
                 pltpu.VMEM((n, 8, HEAD), F32),
-                *[pltpu.VMEM((g[1], d), BF16) for g in GROUPS],
+                *[pltpu.VMEM((rows_in(m)[1], d), BF16) for m in range(len(JOINED))],
                 *[pltpu.VMEM((n_dev, g[1], d), BF16) for g in GROUPS],
-                *[pltpu.VMEM((n_dev, g[1], d), BF16) for g in GROUPS],
+                *[pltpu.VMEM((n_dev, rows_in(m)[1], d), BF16) for m in range(len(JOINED))],
                 pltpu.SemaphoreType.DMA((NK,)),
                 pltpu.SemaphoreType.DMA((NV,)),
                 pltpu.SemaphoreType.DMA((9,)),
-                pltpu.SemaphoreType.DMA((len(GROUPS), 2, n_dev)),
-                pltpu.SemaphoreType.DMA((len(GROUPS), 2, n_dev)),
+                pltpu.SemaphoreType.DMA((len(GROUPS) + len(JOINED), n_dev)),
+                pltpu.SemaphoreType.DMA((len(GROUPS) + len(JOINED), n_dev)),
             ],
             compiler_params=pltpu.CompilerParams(vmem_limit_bytes=56 << 20, collective_id=0, has_side_effects=True),
         )(

time: 104 us -> 102 us (0.981)
  Pallas kernels: 103 us -> 100 us
    pallas_call x1, Pallas kernels: 103 us -> 100 us  [step(): pl.pallas_call(functools.partial(layer, n_dev), out_shape=jax.ShapeDtypeS...]
where the time goes in v6:
time: 102 us
  Pallas kernels  100 us (98%)
  local copies, waits for them, and re-layouts  1.67 us (2%)
    pallas_call x1, Pallas kernels, step(): pl.pallas_call(functools.partial(layer, n_dev), out_shape=jax.ShapeDtypeS...  100 us

profile of v6, /device:TPU:0, one launch (start us, length us, event | category | flops | bytes accessed | tf_op | source)
XLA Modules:
  0.0 102.2 jit_solution(17088173880678629174)
XLA Ops:
  0.0 100.5 %shard_map.109 = bf16[8,8,2048]{2,1,0:T(8,128)(2,1)} custom-call(bf16[8,8,2048]{2,1,0:T(8,128)(2,1)} %bitcast.7, bf16[64,8192,128]{2,1,0:T(8,128)(2,1)} %bitcast.1.k_ref, bf16[64,8192,128]{2,1,0:T(8,128)(2,1)} %bitcast.2.v_ref, bf16[16,128]{1,0:T(8,128)(2,1)} %bitcast.8, bf16[2048,256]{1,0:T(8,128)(2,1)} %wq_ref.1, bf16[256,2048]{1,0:T(8,128)(2,1)} %wo_ref.1, ...), custom_call_target="tpu_custom_call" | custom-call | tf_op jit(solution)/shard_map/pallas_call | solution.py:289
  100.5 1.7 %copy.13 = bf16[64,2048]{1,0:T(8,128)(2,1)} copy(bf16[64,2048]{1,0:T(8,128)(2,1)} %bitcast.6) | data formatting | bytes 524288

commit v7 on v6

--- a/solution.py
+++ b/solution.py
@@ -14,20 +14,20 @@
 LOG2E = 1.4426950408889634
 BLOCK = 8
 NK = NV = 8
-GROUPS = [(0, 16), (16, 16), (32, 16), (48, 8), (56, 4), (60, 2), (62, 2)]
-JOINED = [(0,), (1,), (2,), (3,), (4, 5, 6)]
+GROUPS = [(0, 16), (16, 16), (32, 8), (40, 8), (48, 8), (56, 4), (60, 2), (62, 2)]
+JOINED = [(0,), (1,), (2, 3), (4,), (5, 6, 7)]
+PIECES = [1, 1, 1, 1, 2]
 STREAM = {
     7: [("attended", 0)],
     11: [("through", 0)],
     15: [("attended", 1), ("done", 0)],
-    19: [("through", 1)],
-    23: [("attended", 2), ("done", 1)],
-    26: [("through", 2)],
-    27: [("attended", 3)],
-    29: [("attended", 4)],
+    19: [("through", 1), ("attended", 2)],
+    23: [("attended", 3), ("done", 1)],
+    25: [("through", 2)],
+    27: [("attended", 4)],
 }
-LATE = [("attended", 5)]
-TAIL = [("attended", 6), ("through", 3), ("done", 2), ("through", 4), ("done", 3), ("done", 4)]
+LATE = [[("attended", 5)], [("attended", 6)]]
+TAIL = [("attended", 7), ("through", 3), ("done", 2), ("through", 4), ("done", 3), ("done", 4)]
 
 
 def rows_in(m):
@@ -99,8 +99,8 @@
     q_v, s0_v, s1_v, p0_v, p1_v, seen_v, *rest,
 ):
     a, m = len(GROUPS), len(JOINED)
-    h_v, hterm, yterm = rest[:m], rest[m : m + a], rest[m + a : 2 * m + a]
-    ksem, vsem, wsem, send_sem, recv_sem = rest[2 * m + a :]
+    h_v, hterm, yterm = rest[:m], rest[m : m + a], rest[m + a : m + a + sum(PIECES)]
+    ksem, vsem, wsem, send_sem, recv_sem = rest[m + a + sum(PIECES) :]
     me = lax.axis_index("tp")
     n = k_ref.shape[0]
     block = x_ref.shape[1]
@@ -169,6 +169,10 @@
         seen = jnp.concatenate([seen_v[first : first + count, 0, :], seen_v[first : first + count, 1, :]], 1)
         send(g, hterm[g], jnp.dot(filled(seen), wo_v[...], preferred_element_type=F32))
 
+    def pieces(m):
+        width = x_ref.shape[2] // PIECES[m]
+        return [(sum(PIECES[:m]) + i, pl.ds(i * width, width)) for i in range(PIECES[m])]
+
     def through(m):
         if m == 0:
             for load in (loads[4], *loads[6:]):
@@ -183,14 +187,16 @@
         b = filled(jnp.concatenate(parts, 0))
         gate = jnp.dot(b, wg_v[...], preferred_element_type=F32)
         up = jnp.dot(b, wu_v[...], preferred_element_type=F32)
-        out = jnp.dot((jax.nn.silu(gate) * up).astype(BF16), wd_v[...], preferred_element_type=F32)
-        send(len(GROUPS) + m, yterm[m], out)
+        hidden = (jax.nn.silu(gate) * up).astype(BF16)
+        for at, cols in pieces(m):
+            send(len(GROUPS) + at, yterm[at], jnp.dot(hidden, wd_v[:, cols], preferred_element_type=F32))
 
     def done(m):
         first, count = rows_in(m)
-        y = (h_v[m][...].astype(F32) + summed(len(GROUPS) + m, yterm[m])).astype(BF16)
-        for b in range(count // block):
-            out_ref[first // block + b] = y[b * block : (b + 1) * block]
+        for at, cols in pieces(m):
+            y = (h_v[m][:, cols].astype(F32) + summed(len(GROUPS) + at, yterm[at])).astype(BF16)
+            for b in range(count // block):
+                out_ref[first // block + b, :, cols] = y[b * block : (b + 1) * block]
 
     def run(steps):
         for step, which in steps:
@@ -253,23 +259,25 @@
 
         return carry
 
-    lax.fori_loop(0, n // 2 - 2, pair, 0)
-    for b in range(2):
-        kcopy(n - 2 + b, (n - 2 + b) % NK).wait()
-    for b in range(2):
-        weights_of(score[b], weight[b])
-    for b in range(2):
-        scores_of(q_v, kbuf, score[b], n - 2 + b, (n - 2 + b) % NK)
-    for b in range(2):
-        vcopy(n - 4 + b, (n - 4 + b) % NV).wait()
-    for b in range(2):
-        seen_from(weight[b], vbuf, seen_v, n - 4 + b, (n - 4 + b) % NV)
-    for b in range(2):
-        weights_of(score[b], weight[b])
-    run(LATE)
-    for b in range(2):
-        vcopy(n - 2 + b, (n - 2 + b) % NV).wait()
-        seen_from(weight[b], vbuf, seen_v, n - 2 + b, (n - 2 + b) % NV)
+    lax.fori_loop(0, n // 2 - 3, pair, 0)
+    for i, steps in zip((n - 6, n - 4), LATE):
+        for b in range(i + 2, i + 4):
+            kcopy(b, b % NK).wait()
+        if i == n - 6:
+            for b in range(2):
+                weights_of(score[b], weight[b])
+        for b in range(i + 2, i + 4):
+            scores_of(q_v, kbuf, score[b % 2], b, b % NK)
+        for b in range(i, i + 2):
+            vcopy(b, b % NV).wait()
+        for b in range(i, i + 2):
+            seen_from(weight[b % 2], vbuf, seen_v, b, b % NV)
+        for b in range(2):
+            weights_of(score[b], weight[b])
+        run(steps)
+    for b in range(n - 2, n):
+        vcopy(b, b % NV).wait()
+        seen_from(weight[b % 2], vbuf, seen_v, b, b % NV)
     run(TAIL)
 
 
@@ -311,12 +319,12 @@
                 pltpu.VMEM((n, 8, HEAD), F32),
                 *[pltpu.VMEM((rows_in(m)[1], d), BF16) for m in range(len(JOINED))],
                 *[pltpu.VMEM((n_dev, g[1], d), BF16) for g in GROUPS],
-                *[pltpu.VMEM((n_dev, rows_in(m)[1], d), BF16) for m in range(len(JOINED))],
+                *[pltpu.VMEM((n_dev, rows_in(m)[1], d // c), BF16) for m, c in enumerate(PIECES) for _ in range(c)],
                 pltpu.SemaphoreType.DMA((NK,)),
                 pltpu.SemaphoreType.DMA((NV,)),
                 pltpu.SemaphoreType.DMA((9,)),
-                pltpu.SemaphoreType.DMA((len(GROUPS) + len(JOINED), n_dev)),
-                pltpu.SemaphoreType.DMA((len(GROUPS) + len(JOINED), n_dev)),
+                pltpu.SemaphoreType.DMA((len(GROUPS) + sum(PIECES), n_dev)),
+                pltpu.SemaphoreType.DMA((len(GROUPS) + sum(PIECES), n_dev)),
             ],
             compiler_params=pltpu.CompilerParams(vmem_limit_bytes=56 << 20, collective_id=0, has_side_effects=True),
         )(

time: 102 us -> 101 us (level)
    pallas_call x1, Pallas kernels: 100 us -> 99.2 us  [step(): pl.pallas_call(functools.partial(layer, n_dev), out_shape=jax.ShapeDtypeS...]
where the time goes in v7:
time: 101 us
  Pallas kernels  99.2 us (98%)
  local copies, waits for them, and re-layouts  1.67 us (2%)
    pallas_call x1, Pallas kernels, step(): pl.pallas_call(functools.partial(layer, n_dev), out_shape=jax.ShapeDtypeS...  99.2 us

profile of v7, /device:TPU:0, one launch (start us, length us, event | category | flops | bytes accessed | tf_op | source)
XLA Modules:
  0.0 100.9 jit_solution(13773784087173467336)
XLA Ops:
  0.0 99.2 %shard_map.109 = bf16[8,8,2048]{2,1,0:T(8,128)(2,1)} custom-call(bf16[8,8,2048]{2,1,0:T(8,128)(2,1)} %bitcast.7, bf16[64,8192,128]{2,1,0:T(8,128)(2,1)} %bitcast.1.k_ref, bf16[64,8192,128]{2,1,0:T(8,128)(2,1)} %bitcast.2.v_ref, bf16[16,128]{1,0:T(8,128)(2,1)} %bitcast.8, bf16[2048,256]{1,0:T(8,128)(2,1)} %wq_ref.1, bf16[256,2048]{1,0:T(8,128)(2,1)} %wo_ref.1, ...), custom_call_target="tpu_custom_call" | custom-call | tf_op jit(solution)/shard_map/pallas_call | solution.py:297
  99.2 1.7 %copy.13 = bf16[64,2048]{1,0:T(8,128)(2,1)} copy(bf16[64,2048]{1,0:T(8,128)(2,1)} %bitcast.6) | data formatting | bytes 524288

commit v8 on v7

--- a/solution.py
+++ b/solution.py
@@ -104,7 +104,9 @@
     me = lax.axis_index("tp")
     n = k_ref.shape[0]
     block = x_ref.shape[1]
-    peers = [lax.rem(me + j, n_dev) for j in range(1, n_dev)]
+    bits = [lax.rem(me // (1 << b), 2) for b in range(n_dev.bit_length() - 1)]
+    far = sorted(range(1, n_dev), key=lambda j: (-bin(j >> 1).count("1"), j & 1, -j))
+    peers = [sum(lax.rem(bit + (j >> b), 2) * (1 << b) for b, bit in enumerate(bits)) for j in far]
 
     loads = [
         pltpu.make_async_copy(src, dst, wsem.at[i])

time: 101 us -> 101 us (level)
  no operation moved by 1% of the time
where the time goes in v8:
time: 101 us
  Pallas kernels  99 us (98%)
  local copies, waits for them, and re-layouts  1.67 us (2%)
    pallas_call x1, Pallas kernels, step(): pl.pallas_call(functools.partial(layer, n_dev), out_shape=jax.ShapeDtypeS...  99 us

profile of v8, /device:TPU:0, one launch (start us, length us, event | category | flops | bytes accessed | tf_op | source)
XLA Modules:
  0.0 100.7 jit_solution(9559999877589962813)
XLA Ops:
  0.0 99.0 %shard_map.109 = bf16[8,8,2048]{2,1,0:T(8,128)(2,1)} custom-call(bf16[8,8,2048]{2,1,0:T(8,128)(2,1)} %bitcast.7, bf16[64,8192,128]{2,1,0:T(8,128)(2,1)} %bitcast.1.k_ref, bf16[64,8192,128]{2,1,0:T(8,128)(2,1)} %bitcast.2.v_ref, bf16[16,128]{1,0:T(8,128)(2,1)} %bitcast.8, bf16[2048,256]{1,0:T(8,128)(2,1)} %wq_ref.1, bf16[256,2048]{1,0:T(8,128)(2,1)} %wo_ref.1, ...), custom_call_target="tpu_custom_call" | custom-call | tf_op jit(solution)/shard_map/pallas_call | solution.py:299
  99.0 1.7 %copy.13 = bf16[64,2048]{1,0:T(8,128)(2,1)} copy(bf16[64,2048]{1,0:T(8,128)(2,1)} %bitcast.6) | data formatting | bytes 524288
